TPU v7x, 16 devices: a 4x2x1 block of a 4x4x8 slice. The times are simulated.
16 devices in a mesh: stage: 2 (over y, z), data: 8 (over x, core).
Axes of the slice: x: 4, y: 2, z: 1, core: 2. Of those that a mesh axis runs over, the one named last changes fastest.
The devices are a block of a 4x4x8 slice.
Arguments:
- w_master: float32 [48, 2048, 1024], P('stage', 'data'), parts along dimension 0
- momentum: float32 [48, 2048, 1024], P('stage', 'data'), parts along dimension 0
- grad: bfloat16 [48, 2048, 1024], P('stage', 'data'), parts along dimension 0
Outputs:
- output 1: bfloat16 [48, 2048, 1024], P('stage'), parts along dimension 0
- output 2: float32 [48, 2048, 1024], P('stage', 'data'), parts along dimension 0
There are 2 independent parts. A program takes and returns all parts, laid end to end along the dimension named above; each array names one.
All inputs are finite; a program needn't handle non-finite values.
Results may differ from a plain program's by a relative error of at most 0.00729924.
Values are sent between devices in bfloat16 or wider.
A program may use at most 768 MiB of HBM per device.

v0:
```python
import math
import jax
import jax.numpy as jnp
from jax import lax
from jax.sharding import PartitionSpec as P

NS_ITERS = 5
MOMENTUM = 0.95
LEARN_RATE = 0.02
WEIGHT_DECAY = 0.1
NORM_EPS = 1e-7
COEF_A = 3.4445
COEF_B = -4.7750
COEF_C = 2.0315


def newton_schulz(x_mat):
    wide = x_mat.shape[1] <= x_mat.shape[2]
    for iteration in range(NS_ITERS):
        if wide:
            gram_mat = jnp.einsum("kip,kjp->kij", x_mat, x_mat, preferred_element_type=jnp.float32)
        else:
            gram_mat = jnp.einsum("kpi,kpj->kij", x_mat, x_mat, preferred_element_type=jnp.float32)
        gram_mat = gram_mat.astype(jnp.bfloat16)
        square = jnp.einsum("kij,kjl->kil", gram_mat, gram_mat, preferred_element_type=jnp.float32)
        poly_mat = (COEF_B * gram_mat.astype(jnp.float32) + COEF_C * square).astype(jnp.bfloat16)
        if wide:
            prod_mat = jnp.einsum("kij,kjp->kip", poly_mat, x_mat, preferred_element_type=jnp.float32)
        else:
            prod_mat = jnp.einsum("kpj,kij->kpi", x_mat, poly_mat, preferred_element_type=jnp.float32)
        x_mat = (COEF_A * x_mat.astype(jnp.float32) + prod_mat).astype(jnp.bfloat16)
    return x_mat


def solution(mesh):
    group = mesh.shape["data"]
    row_spec = P("stage", "data", None)
    full_spec = P("stage", None, None)

    def local_step(w_rows, mom_rows, grad_rows):
        mat_count, rows_dev, col_count = mom_rows.shape
        own_count = mat_count // group
        rms_scale = 0.2 * math.sqrt(max(rows_dev * group, col_count))
        mom_new = MOMENTUM * mom_rows + grad_rows.astype(jnp.float32)
        sq_total = lax.psum(jnp.sum(mom_new * mom_new, axis=(1, 2)), "data")
        owned = lax.all_to_all(mom_new.astype(jnp.bfloat16), "data", 0, 1, tiled=True)
        my_index = lax.axis_index("data")
        sq_owned = lax.dynamic_slice_in_dim(sq_total, my_index * own_count, own_count)
        x_mat = (owned.astype(jnp.float32) / (jnp.sqrt(sq_owned)[:, None, None] + NORM_EPS)).astype(jnp.bfloat16)
        x_mat = newton_schulz(x_mat)
        ortho_rows = lax.all_to_all(x_mat, "data", 1, 0, tiled=True)
        w_new = w_rows - LEARN_RATE * (ortho_rows.astype(jnp.float32) * rms_scale + WEIGHT_DECAY * w_rows)
        params = lax.all_gather(w_new.astype(jnp.bfloat16), "data", axis=1, tiled=True)
        return params, mom_new

    return jax.shard_map(local_step, mesh=mesh, in_specs=(row_spec, row_spec, row_spec), out_specs=(full_spec, row_spec), check_vma=False)
```

profile of v0, /device:TPU:113, one launch (start us, length us, event | category | flops | bytes accessed | tf_op | source)
XLA Modules:
  0.0 1246.6 jit_solution(15691215071859189271)
XLA Ops:
  7.2 14.2 %multiply_reduce_fusion = (f32[24]{0:T(128)S(1)}, f32[24,256,1024]{2,1,0:T(8,128)S(1)}) fusion(bf16[24,256,1024]{2,1,0:T(8,128)(2,1)} %param.5, f32[24,256,1024]{2,1,0:T(8,128)} %param.4), kind=kLoop, calls=%fused_computation.12 | loop fusion | flops 31457256 | bytes 62914656 | tf_op jit(solution)/shard_map/reduce_sum | solution.py:45
  21.4 0.0 copy-start
  21.4 8.9 copy-done
  30.3 5.7 convert_element_type.106
  36.0 6.0 all-to-all-start
  42.1 0.0 all-gather.2.cloned.1.call-start
  42.1 143.1 %psum.7 = f32[24]{0:T(128)S(1)} all-reduce(f32[24]{0:T(128)S(1)} %get-tuple-element.2), channel_id=1, replica_groups=mesh['stage'=2,'data'=8] {'data'}, use_global_device_ids=true, to_apply=%region_1.0 | all-reduce | flops 24 | bytes 192 | tf_op jit(solution)/shard_map/psum | solution.py:45
  185.1 0.1 sqrt_add_fusion
  185.2 0.0 all-to-all-done
  185.2 7.1 copy.12
  192.3 7.7 fusion
  200.0 21.5 %convolution_convert_fusion.4 = bf16[3,1024,1024]{2,1,0:T(8,128)(2,1)} fusion(bf16[3,2048,1024]{2,1,0:T(8,128)(2,1)} %fusion), kind=kOutput, calls=%fused_computation.33 | convolution fusion | flops 12888047616 | bytes 18874368 | tf_op jit(solution)/shard_map/kpi,kpj->kij/dot_general | solution.py:23
  221.5 33.5 %add_convert_fusion.4 = bf16[3,2048,1024]{2,1,0:T(8,128)(2,1)} fusion(bf16[3,2048,1024]{2,1,0:T(8,128)(2,1)} %fusion, bf16[3,1024,1024]{2,1,0:T(8,128)(2,1)} %convolution_convert_fusion.4), kind=kOutput, calls=%fused_computation.11 | convolution fusion | flops 19368247296 | bytes 31457280 | tf_op jit(solution)/shard_map/kpj,kij->kpi/dot_general | solution.py:30
  255.0 21.7 %convolution_convert_fusion.3 = bf16[3,1024,1024]{2,1,0:T(8,128)(2,1)} fusion(bf16[3,2048,1024]{2,1,0:T(8,128)(2,1)} %add_convert_fusion.4), kind=kOutput, calls=%fused_computation.32 | convolution fusion | flops 12888047616 | bytes 18874368 | tf_op jit(solution)/shard_map/kpi,kpj->kij/dot_general | solution.py:23
  276.7 33.6 %add_convert_fusion.3 = bf16[3,2048,1024]{2,1,0:T(8,128)(2,1)} fusion(bf16[3,2048,1024]{2,1,0:T(8,128)(2,1)} %add_convert_fusion.4, bf16[3,1024,1024]{2,1,0:T(8,128)(2,1)} %convolution_convert_fusion.3), kind=kOutput, calls=%fused_computation.10 | convolution fusion | flops 19368247296 | bytes 31457280 | tf_op jit(solution)/shard_map/kpj,kij->kpi/dot_general | solution.py:30
  310.3 22.0 %convolution_convert_fusion.2 = bf16[3,1024,1024]{2,1,0:T(8,128)(2,1)} fusion(bf16[3,2048,1024]{2,1,0:T(8,128)(2,1)} %add_convert_fusion.3), kind=kOutput, calls=%fused_computation.31 | convolution fusion | flops 12888047616 | bytes 18874368 | tf_op jit(solution)/shard_map/kpi,kpj->kij/dot_general | solution.py:23
  332.3 33.4 %add_convert_fusion.2 = bf16[3,2048,1024]{2,1,0:T(8,128)(2,1)} fusion(bf16[3,2048,1024]{2,1,0:T(8,128)(2,1)} %add_convert_fusion.3, bf16[3,1024,1024]{2,1,0:T(8,128)(2,1)} %convolution_convert_fusion.2), kind=kOutput, calls=%fused_computation.9 | convolution fusion | flops 19368247296 | bytes 31457280 | tf_op jit(solution)/shard_map/kpj,kij->kpi/dot_general | solution.py:30
  365.7 21.7 %convolution_convert_fusion.1 = bf16[3,1024,1024]{2,1,0:T(8,128)(2,1)} fusion(bf16[3,2048,1024]{2,1,0:T(8,128)(2,1)} %add_convert_fusion.2), kind=kOutput, calls=%fused_computation.30 | convolution fusion | flops 12888047616 | bytes 18874368 | tf_op jit(solution)/shard_map/kpi,kpj->kij/dot_general | solution.py:23
  387.4 33.5 %add_convert_fusion.1 = bf16[3,2048,1024]{2,1,0:T(8,128)(2,1)} fusion(bf16[3,2048,1024]{2,1,0:T(8,128)(2,1)} %add_convert_fusion.2, bf16[3,1024,1024]{2,1,0:T(8,128)(2,1)} %convolution_convert_fusion.1), kind=kOutput, calls=%fused_computation.8 | convolution fusion | flops 19368247296 | bytes 31457280 | tf_op jit(solution)/shard_map/kpj,kij->kpi/dot_general | solution.py:30
  420.9 21.8 %convolution_convert_fusion = bf16[3,1024,1024]{2,1,0:T(8,128)(2,1)} fusion(bf16[3,2048,1024]{2,1,0:T(8,128)(2,1)} %add_convert_fusion.1), kind=kOutput, calls=%fused_computation.29 | convolution fusion | flops 12888047616 | bytes 18874368 | tf_op jit(solution)/shard_map/kpi,kpj->kij/dot_general | solution.py:23
  442.6 33.8 %add_convert_fusion = bf16[3,2048,1024]{2,1,0:T(8,128)(2,1)} fusion(bf16[3,2048,1024]{2,1,0:T(8,128)(2,1)} %add_convert_fusion.1, bf16[3,1024,1024]{2,1,0:T(8,128)(2,1)} %convolution_convert_fusion), kind=kOutput, calls=%fused_computation.7 | convolution fusion | flops 19368247296 | bytes 31457280 | tf_op jit(solution)/shard_map/kpj,kij->kpi/dot_general | solution.py:30
  476.4 17.9 %copy.18 = bf16[3,2048,1024]{2,0,1:T(4,128)(2,1)S(1)} copy(bf16[3,2048,1024]{2,1,0:T(8,128)(2,1)} %add_convert_fusion) | data formatting | bytes 25165824 | tf_op jit(solution)/shard_map/convert_element_type | solution.py:31
  494.3 189.2 %all_to_all.8 = bf16[3,2048,1024]{2,0,1:T(4,128)(2,1)} all-to-all(bf16[3,2048,1024]{2,0,1:T(4,128)(2,1)S(1)} %copy.18), channel_id=1, replica_groups=mesh['stage'=2,'data'=8] {'data'}, dimensions={1} | all-to-all | bytes 25165824 | tf_op jit(solution)/shard_map/all_to_all | solution.py:51
  683.5 15.9 %convert_multiply_fusion = f32[3,2048,1024]{2,0,1:T(4,128)} fusion(bf16[3,2048,1024]{2,0,1:T(4,128)(2,1)} %all_to_all.8), kind=kLoop, calls=%fused_computation | loop fusion | flops 12582912 | bytes 37748736 | tf_op jit(solution)/shard_map/mul | solution.py:52
  699.4 22.9 %copy.19 = f32[8,3,256,1024]{3,2,1,0:T(8,128)S(1)} copy(f32[8,3,256,1024]{3,1,2,0:T(4,128)} %bitcast.44) | data formatting | bytes 50331648 | tf_op jit(solution)/shard_map/mul | solution.py:52
  722.2 15.5 %fusion.3 = bf16[24,256,1024]{2,1,0:T(8,128)(2,1)} fusion(f32[24,256,1024]{2,1,0:T(8,128)} %param.3, f32[8,3,256,1024]{3,2,1,0:T(8,128)S(1)} %copy.19), kind=kLoop, calls=%fused_computation.6 | loop fusion | flops 31457280 | bytes 62914560 | tf_op jit(solution)/shard_map/convert_element_type | solution.py:53
  737.7 0.1 all-gather.2.cloned.1.call-update
  737.8 435.7 %all-gather.2.cloned.1.call-done = bf16[24,2048,1024]{2,1,0:T(8,128)(2,1)} async-done(((bf16[24,256,1024]{2,1,0:T(8,128)(2,1)}), bf16[24,2048,1024]{2,1,0:T(8,128)(2,1)}) %all-gather.2.cloned.1.call-update) | async-done | bytes 100663312 | tf_op jit(solution)/shard_map/all_gather | solution.py:53
  1173.5 66.1 %copy.26 = bf16[24,2048,1024]{2,1,0:T(8,128)(2,1)} copy(bf16[24,2048,1024]{2,1,0:T(8,128)(2,1)} %all-gather.2.cloned.1.call-done) | data formatting | bytes 201326592
Async XLA Ops:
  21.4 8.9 copy-start
  36.0 149.2 %all-to-all-start = ((bf16[24,256,1024]{2,1,0:T(8,128)(2,1)}), bf16[24,256,1024]{2,1,0:T(8,128)(2,1)}, u32[]{:S(2)}, u32[]{:S(2)}) async-start(bf16[24,256,1024]{2,1,0:T(8,128)(2,1)} %convert_element_type.106), calls=%async_computation | async-start | bytes 25165824 | tf_op jit(solution)/shard_map/all_to_all | solution.py:46
  42.1 1131.4 %all-gather.2.cloned.1.call-start = ((), (), s32[]{:S(2)}) async-start(), calls=%async_computation.2 | async-start | bytes 113246208 | tf_op jit(solution)/shard_map/all_gather | solution.py:53
Sparse Core Ops, SparseCore 0:
  737.9 435.5 all-gather.1
where the time goes:
time: 1250 us
  waiting for transfers between devices  436 us (35%)
  blocking collectives  332 us (27%)
  matrix products  276 us (22%)
  local copies, waits for them, and re-layouts  123 us (10%)
  other arithmetic  59.1 us (5%)
  between operations  14.3 us (1%)
    all_gather x1, waiting for transfers between devices, local_step(): lax.all_gather(w_new.astype(jnp.bfloat16), 'data', axis=1, tiled=True)  436 us
    all_to_all x1, blocking collectives, local_step(): ortho_rows = lax.all_to_all(x_mat, 'data', 1, 0, tiled=True)  189 us
    dot_general x5, matrix products, newton_schulz(): jnp.einsum('kpj,kij->kpi', x_mat, poly_mat, preferred_element_type=jnp.fl...  168 us
    psum x1, blocking collectives, local_step(): sq_total = lax.psum(jnp.sum(mom_new * mom_new, axis=(1, 2)), 'data')  143 us
    dot_general x5, matrix products, newton_schulz(): jnp.einsum('kpi,kpj->kij', x_mat, x_mat, preferred_element_type=jnp.float32)  109 us
    unnamed x3, local copies, waits for them, and re-layouts  75 us
  transfers between devices with their start and end apart: 2, of which 1 were waited for; matrix products, arithmetic and copies ran while one was open for 0% of the time, Pallas kernels for 0%

commit v1 on v0

v1 whole, which is shorter than its diff:
```python
import functools
import math

import jax
import jax.numpy as jnp
from jax import lax
from jax.experimental import pallas as pl
from jax.experimental.pallas import tpu as pltpu
from jax.sharding import PartitionSpec as P

NS_ITERS = 5
MOMENTUM = 0.95
LEARN_RATE = 0.02
WEIGHT_DECAY = 0.1
NORM_EPS = 1e-7
COEF_A = 3.4445
COEF_B = -4.7750
COEF_C = 2.0315

MESH = pl.DeviceIdType.MESH
CORES = 2
BLK = 256
CHUNK = 32
VMEM_LIMIT = 60 * 1024 * 1024
F32 = jnp.float32
BF16 = jnp.bfloat16


def aligned(start, size):
    return pl.ds(pl.multiple_of(start, size), size)


def step_offsets(k, chips):
    return lax.rem(k // CORES + 1, chips), lax.rem(k, CORES)


def target_of(me, k, chips):
    dx, dc = step_offsets(k, chips)
    return lax.rem(me // CORES + dx, chips) * CORES + lax.rem(lax.rem(me, CORES) + dc, CORES)


def source_of(me, k, chips):
    dx, dc = step_offsets(k, chips)
    return lax.rem(me // CORES + chips - dx, chips) * CORES + lax.rem(lax.rem(me, CORES) + dc, CORES)


def greet_group(me, group, chips):
    barrier = pltpu.get_barrier_semaphore()
    for k in range(group):
        if k != group - CORES:
            pl.semaphore_signal(barrier, inc=1, device_id={"data": target_of(me, k, chips)}, device_id_type=MESH)
    pl.semaphore_wait(barrier, group - 1)


def newton_schulz(y, gram, poly):
    rows, cols = y.shape

    def iteration(_, carry):
        def gram_block(i, c):
            at = aligned(i * BLK, BLK)
            gram[at, :] = lax.dot_general(y[:, at], y[...], (((0,), (0,)), ((), ())), preferred_element_type=F32).astype(BF16)
            return c

        def poly_block(i, c):
            at = aligned(i * BLK, BLK)
            part = gram[at, :]
            square = jnp.dot(part, gram[...], preferred_element_type=F32)
            poly[at, :] = (COEF_B * part.astype(F32) + COEF_C * square).astype(BF16)
            return c

        def update_block(i, c):
            at = aligned(i * BLK, BLK)
            part = y[at, :]
            prod = jnp.dot(part, poly[...], preferred_element_type=F32)
            y[at, :] = (COEF_A * part.astype(F32) + prod).astype(BF16)
            return c

        lax.fori_loop(0, cols // BLK, gram_block, 0)
        lax.fori_loop(0, cols // BLK, poly_block, 0)
        lax.fori_loop(0, rows // BLK, update_block, 0)
        return carry

    lax.fori_loop(0, NS_ITERS, iteration, 0)


def start_weights(me, wave, group, w_hbm, w_vmem, w_sem, chips):
    def load(k, c):
        owner = source_of(me, k, chips)
        pltpu.make_async_copy(w_hbm.at[wave * group + owner], w_vmem.at[k], w_sem.at[k]).start()
        return c

    lax.fori_loop(0, group, load, 0)


def orthogonalize_wave(me, wave, group, chips, land, norms, w_hbm, w_out, y, gram, poly, norm_v, x_land, w_vmem, o_vmem,
                       y_sem, x_send, x_recv, w_sem, o_sem):
    rows, cols = y.shape
    rows_dev = rows // group
    own_k = group - CORES
    scale = 0.2 * math.sqrt(max(rows, cols))

    load_y = pltpu.make_async_copy(land.at[wave], y, y_sem.at[0])
    load_n = pltpu.make_async_copy(norms.at[wave], norm_v, y_sem.at[1])
    load_y.start()
    load_n.start()
    load_y.wait()
    load_n.wait()
    total = jnp.sum(jnp.sum(norm_v[...], axis=0), axis=(0, 1), keepdims=True)
    denom = jnp.sqrt(total) + NORM_EPS

    def normalise(i, c):
        at = aligned(i * CHUNK, CHUNK)
        y[at, :] = (y[at, :].astype(F32) / denom).astype(BF16)
        return c

    lax.fori_loop(0, rows // CHUNK, normalise, 0)
    newton_schulz(y, gram, poly)

    def row_copy(k):
        target = target_of(me, k, chips)
        return pltpu.make_async_remote_copy(
            src_ref=y.at[aligned(target * rows_dev, rows_dev)],
            dst_ref=x_land.at[k],
            send_sem=x_send.at[k],
            recv_sem=x_recv.at[k],
            device_id={"data": target},
            device_id_type=MESH,
        )

    for k in range(group):
        if k != own_k:
            row_copy(k).start()
    own = pltpu.make_async_copy(y.at[aligned(me * rows_dev, rows_dev)], x_land.at[own_k], y_sem.at[0])
    own.start()

    def update(j, c):
        k = lax.rem(j + own_k, group)
        owner = source_of(me, k, chips)
        pltpu.make_async_copy(w_hbm.at[wave * group + owner], w_vmem.at[k], w_sem.at[k]).wait()

        @pl.when(k == own_k)
        def _():
            own.wait()

        @pl.when(k != own_k)
        def _():
            row_copy(k).wait_recv()

        def chunk(i, c2):
            at = aligned(i * CHUNK, CHUNK)
            w_old = w_vmem[k, at, :]
            ortho = x_land[k, at, :].astype(F32) * scale
            o_vmem[k, at, :] = (w_old - LEARN_RATE * (ortho + WEIGHT_DECAY * w_old)).astype(BF16)
            return c2

        lax.fori_loop(0, rows_dev // CHUNK, chunk, 0)
        pltpu.make_async_copy(o_vmem.at[k], w_out.at[owner], o_sem.at[k]).start()
        return c

    lax.fori_loop(0, group, update, 0)

    def finish(k, c):
        owner = source_of(me, k, chips)
        pltpu.make_async_copy(o_vmem.at[k], w_out.at[owner], o_sem.at[k]).wait()

        @pl.when(k != own_k)
        def _():
            row_copy(k).wait_send()

        return c

    lax.fori_loop(0, group, finish, 0)


def first_kernel(group, waves, mom, grad, w_hbm, w_out, land, norms, send, norm_send, mom_v, grad_v, load_sem, m_send, m_recv,
                 n_send, n_recv, l_sem, *work):
    me = lax.axis_index("data")
    chips = group // CORES
    own_k = group - CORES
    rows_dev, cols = mom.shape[1:]
    steps = waves * group
    greet_group(me, group, chips)
    y, gram, poly, norm_v, x_land, w_vmem, o_vmem, y_sem, x_send, x_recv, w_sem, o_sem = work
    mine = aligned(me * rows_dev, rows_dev)

    def loads(t):
        wave, k = t // group, lax.rem(t, group)
        mat = wave * group + target_of(me, k, chips)
        slot = lax.rem(t, 2)
        return (
            pltpu.make_async_copy(mom.at[mat], mom_v.at[slot], load_sem.at[0, slot]),
            pltpu.make_async_copy(grad.at[mat], grad_v.at[slot], load_sem.at[1, slot]),
        )

    def remote(wave, k):
        target = target_of(me, k, chips)
        t = wave * group + k
        rows = pltpu.make_async_remote_copy(
            src_ref=send.at[t], dst_ref=land.at[wave, mine], send_sem=m_send.at[wave, k], recv_sem=m_recv.at[wave, k],
            device_id={"data": target}, device_id_type=MESH)
        norm = pltpu.make_async_remote_copy(
            src_ref=norm_send.at[t], dst_ref=norms.at[wave, me], send_sem=n_send.at[wave, k], recv_sem=n_recv.at[wave, k],
            device_id={"data": target}, device_id_type=MESH)
        return rows, norm

    def local(wave):
        t = wave * group + own_k
        return (
            pltpu.make_async_copy(send.at[t], land.at[wave, mine], l_sem.at[0, wave]),
            pltpu.make_async_copy(norm_send.at[t], norms.at[wave, me], l_sem.at[1, wave]),
        )

    def dispatch(t):
        wave, k = t // group, lax.rem(t, group)

        @pl.when(k == own_k)
        def _():
            for copy in local(wave):
                copy.start()

        @pl.when(k != own_k)
        def _():
            for copy in remote(wave, k):
                copy.start()

    for copy in loads(0):
        copy.start()

    def form(t, c):
        @pl.when(t + 1 < steps)
        def _():
            for copy in loads(t + 1):
                copy.start()

        for copy in loads(t):
            copy.wait()
        slot = lax.rem(t, 2)

        def chunk(i, acc):
            at = aligned(i * CHUNK, CHUNK)
            new = MOMENTUM * mom_v[slot, at, :] + grad_v[slot, at, :].astype(F32)
            send[t, at, :] = new.astype(BF16)
            sq = new * new
            for r in range(0, CHUNK, 8):
                acc = acc + sq[r:r + 8, :]
            return acc

        acc = lax.fori_loop(0, rows_dev // CHUNK, chunk, jnp.zeros((8, cols), F32))
        part = acc[:, 0:128]
        for col in range(128, cols, 128):
            part = part + acc[:, col:col + 128]
        norm_send[t] = part

        @pl.when(t > 0)
        def _():
            dispatch(t - 1)

        return c

    lax.fori_loop(0, steps, form, 0)
    dispatch(jnp.int32(steps - 1))
    start_weights(me, 0, group, w_hbm, w_vmem, w_sem, chips)

    def arrived(wave):
        for k in range(group):
            if k != own_k:
                for copy in remote(wave, k):
                    copy.wait_recv()
        for copy in local(wave):
            copy.wait()

    arrived(0)
    orthogonalize_wave(me, 0, group, chips, land, norms, w_hbm, w_out, *work)
    for wave in range(1, waves):
        arrived(wave)
    for wave in range(waves):
        for k in range(group):
            if k != own_k:
                for copy in remote(wave, k):
                    copy.wait_send()


def later_kernel(group, wave, land, norms, w_hbm, w_out, *work):
    me = lax.axis_index("data")
    chips = group // CORES
    greet_group(me, group, chips)
    start_weights(me, wave, group, w_hbm, work[5], work[10], chips)
    orthogonalize_wave(me, wave, group, chips, land, norms, w_hbm, w_out, *work)


def momentum_kernel(mom, grad, _, out):
    out[...] = MOMENTUM * mom[...] + grad[...].astype(F32)


def place_kernel(src, *refs):
    refs[-1][...] = src[0]


def solution(mesh):
    group = mesh.shape["data"]
    row_spec = P("stage", "data", None)
    full_spec = P("stage", None, None)
    any_spec = pl.BlockSpec(memory_space=pl.ANY)

    def local_step(w_rows, mom_rows, grad_rows):
        mats, rows_dev, cols = mom_rows.shape
        rows = rows_dev * group
        waves = mats // group
        ns_flops = NS_ITERS * 2 * (2 * rows * cols * cols + cols**3)
        work = [
            pltpu.VMEM((rows, cols), BF16),
            pltpu.VMEM((cols, cols), BF16),
            pltpu.VMEM((cols, cols), BF16),
            pltpu.VMEM((group, 8, 128), F32),
            pltpu.VMEM((group, rows_dev, cols), BF16),
            pltpu.VMEM((group, rows_dev, cols), F32),
            pltpu.VMEM((group, rows_dev, cols), BF16),
            pltpu.SemaphoreType.DMA((2,)),
            pltpu.SemaphoreType.DMA((group,)),
            pltpu.SemaphoreType.DMA((group,)),
            pltpu.SemaphoreType.DMA((group,)),
            pltpu.SemaphoreType.DMA((group,)),
        ]
        w_new_shape = jax.ShapeDtypeStruct((group, rows_dev, cols), BF16)
        cost = pl.CostEstimate(flops=ns_flops, bytes_accessed=8 * rows * cols, transcendentals=0)
        w_new, land, norms = pl.pallas_call(
            functools.partial(first_kernel, group, waves),
            name="first_wave",
            out_shape=(
                w_new_shape,
                jax.ShapeDtypeStruct((waves, rows, cols), BF16),
                jax.ShapeDtypeStruct((waves, group, 8, 128), F32),
            ),
            in_specs=[any_spec] * 3,
            out_specs=(any_spec,) * 3,
            scratch_shapes=[
                pltpu.VMEM((mats, rows_dev, cols), BF16),
                pltpu.VMEM((mats, 8, 128), F32),
                pltpu.VMEM((2, rows_dev, cols), F32),
                pltpu.VMEM((2, rows_dev, cols), BF16),
                pltpu.SemaphoreType.DMA((2, 2)),
                pltpu.SemaphoreType.DMA((waves, group)),
                pltpu.SemaphoreType.DMA((waves, group)),
                pltpu.SemaphoreType.DMA((waves, group)),
                pltpu.SemaphoreType.DMA((waves, group)),
                pltpu.SemaphoreType.DMA((2, waves)),
                *work,
            ],
            compiler_params=pltpu.CompilerParams(collective_id=0, has_side_effects=True, vmem_limit_bytes=VMEM_LIMIT),
            cost_estimate=cost,
        )(mom_rows, grad_rows, w_rows)
        gathered = [lax.all_gather(w_new, "data", axis=0)]
        for wave in range(1, waves):
            w_new = pl.pallas_call(
                functools.partial(later_kernel, group, wave),
                name=f"wave_{wave}",
                out_shape=w_new_shape,
                in_specs=[any_spec] * 3,
                out_specs=any_spec,
                scratch_shapes=work,
                compiler_params=pltpu.CompilerParams(collective_id=wave, has_side_effects=True, vmem_limit_bytes=VMEM_LIMIT),
                cost_estimate=cost,
            )(land, norms, w_rows)
            gathered.append(lax.all_gather(w_new, "data", axis=0))
        mom_new = pl.pallas_call(
            momentum_kernel,
            name="momentum",
            grid=(mats,),
            out_shape=jax.ShapeDtypeStruct(mom_rows.shape, F32),
            in_specs=[
                pl.BlockSpec((1, rows_dev, cols), lambda i: (i, 0, 0)),
                pl.BlockSpec((1, rows_dev, cols), lambda i: (i, 0, 0)),
                any_spec,
            ],
            out_specs=pl.BlockSpec((1, rows_dev, cols), lambda i: (i, 0, 0)),
            cost_estimate=pl.CostEstimate(flops=mats * rows_dev * cols * 100, bytes_accessed=10 * mats * rows_dev * cols, transcendentals=0),
        )(mom_rows, grad_rows, w_new)
        params = mom_new
        for wave in range(waves):
            params = pl.pallas_call(
                place_kernel,
                name=f"place_{wave}",
                grid=(group, group),
                out_shape=jax.ShapeDtypeStruct((mats, rows, cols), BF16),
                in_specs=[pl.BlockSpec((1, 1, rows_dev, cols), lambda o, d: (d, o, 0, 0)), any_spec],
                out_specs=pl.BlockSpec((1, rows_dev, cols), lambda o, d, wave=wave: (wave * group + o, d, 0)),
                input_output_aliases={1: 0} if wave else {},
                cost_estimate=pl.CostEstimate(flops=group * rows * cols * 40, bytes_accessed=4 * group * rows * cols, transcendentals=0),
            )(gathered[wave], params)
        return params, mom_new

    return jax.shard_map(local_step, mesh=mesh, in_specs=(row_spec,) * 3, out_specs=(full_spec, row_spec), check_vma=False)
```

time: 1250 us -> 809 us (0.65)
  Pallas kernels: 0 us -> 695 us
  waiting for transfers between devices: 436 us -> 96 us
  blocking collectives: 332 us -> 0 us
  matrix products: 276 us -> 0 us
  local copies, waits for them, and re-layouts: 123 us -> 0 us
  other arithmetic: 59.1 us -> 0 us
    pallas_call x0 -> x7, Pallas kernels: none -> 695 us  [the longest x2 344 us: local_step(): pl.pallas_call(functools.partial(later_kernel, group, wave), name=f'wave_...]
    all_gather x1 -> x3, waiting for transfers between devices: 436 us -> 95.8 us  [the longest x2 95.8 us: local_step(): gathered.append(lax.all_gather(w_new, 'data', axis=0))]
    dot_general x10 -> x0, matrix products: 276 us -> none  [the longest x5 168 us: newton_schulz(): jnp.einsum('kpj,kij->kpi', x_mat, poly_mat, preferred_element_type=jnp.fl...]
    all_to_all x1 -> x0, blocking collectives: 189 us -> none  [local_step(): ortho_rows = lax.all_to_all(x_mat, 'data', 1, 0, tiled=True)]
    psum x1 -> x0, blocking collectives: 143 us -> none  [local_step(): sq_total = lax.psum(jnp.sum(mom_new * mom_new, axis=(1, 2)), 'data')]
    unnamed x3 -> x0, local copies, waits for them, and re-layouts: 75 us -> none
    convert_element_type x3 -> x0, other arithmetic: 28.9 us -> none  [the longest x1 15.5 us: local_step(): w_new.astype(jnp.bfloat16)]
    convert_element_type x2 -> x0, local copies, waits for them, and re-layouts: 25 us -> none  [the longest x1 17.9 us: newton_schulz(): x_mat = (COEF_A * x_mat.astype(jnp.float32) + prod_mat).astype(jnp.bfloat16)]
  transfers between devices with their start and end apart: 2 -> 3, of which waited for: 1 -> 1; matrix products, arithmetic and copies ran while one was open for 0% -> 0% of each run, Pallas kernels for 0% -> 57%
where the time goes in v1:
time: 809 us; the launch traced here: 805 us
  Pallas kernels  695 us (86%)
  waiting for transfers between devices  96 us (12%)
  between operations  13.8 us (2%)
    pallas_call x2, Pallas kernels, local_step(): pl.pallas_call(functools.partial(later_kernel, group, wave), name=f'wave_...  344 us
    pallas_call x1, Pallas kernels, local_step(): pl.pallas_call(functools.partial(first_kernel, group, waves), name='first...  193 us
    pallas_call x3, Pallas kernels, local_step(): pl.pallas_call(place_kernel, name=f'place_{wave}', grid=(group, group), o...  129 us
    all_gather x2, waiting for transfers between devices, local_step(): gathered.append(lax.all_gather(w_new, 'data', axis=0))  95.8 us
    pallas_call x1, Pallas kernels, local_step(): pl.pallas_call(momentum_kernel, name='momentum', grid=(mats,), out_shape=...  28.3 us
  transfers between devices with their start and end apart: 3, of which 1 were waited for; matrix products, arithmetic and copies ran while one was open for 0% of the time, Pallas kernels for 57%

profile of v1, /device:TPU:113, one launch (start us, length us, event | category | flops | bytes accessed | tf_op | source)
XLA Modules:
  0.0 805.1 jit_solution(9688779900850332874)
XLA Ops:
  7.2 0.1 all-gather.11.cloned.1.call-start
  7.2 193.3 %first_wave.1 = (bf16[8,256,1024]{2,1,0:T(8,128)(2,1)}, bf16[3,2048,1024]{2,1,0:T(8,128)(2,1)}, f32[3,8,8,128]{3,2,1,0:T(8,128)}) custom-call(f32[24,256,1024]{2,1,0:T(8,128)} %mom.3, bf16[24,256,1024]{2,1,0:T(8,128)(2,1)} %grad.3, f32[24,256,1024]{2,1,0:T(8,128)} %w_hbm.5), custom_call_target="tpu_custom_call" | custom-call | flops 53687091200 | bytes 16777216 | tf_op jit(solution)/shard_map/first_wave/pallas_call | solution.py:326
  200.5 0.1 all-gather.11.cloned.1.call-update
  200.6 0.1 all-gather.9.cloned.1.call-start
  200.7 172.6 %wave_1.1 = bf16[8,256,1024]{2,1,0:T(8,128)(2,1)} custom-call(bf16[3,2048,1024]{2,1,0:T(8,128)(2,1)} %get-tuple-element.5.land, f32[3,8,8,128]{3,2,1,0:T(8,128)} %get-tuple-element.6.norms, f32[24,256,1024]{2,1,0:T(8,128)} %w_hbm.5), custom_call_target="tpu_custom_call" | custom-call | flops 53687091200 | bytes 16777216 | tf_op jit(solution)/shard_map/wave_1/pallas_call | solution.py:354
  373.3 0.1 all-gather.9.cloned.1.call-update
  373.3 0.1 all-gather.7.cloned.1.call-start
  373.4 171.7 %wave_2.1._ = bf16[8,256,1024]{2,1,0:T(8,128)(2,1)} custom-call(bf16[3,2048,1024]{2,1,0:T(8,128)(2,1)} %get-tuple-element.5.land, f32[3,8,8,128]{3,2,1,0:T(8,128)} %get-tuple-element.6.norms, f32[24,256,1024]{2,1,0:T(8,128)} %w_hbm.5), custom_call_target="tpu_custom_call" | custom-call | flops 53687091200 | bytes 16777216 | tf_op jit(solution)/shard_map/wave_2/pallas_call | solution.py:354
  545.1 0.1 all-gather.7.cloned.1.call-update
  545.2 28.3 %momentum.1.refs_0_ = f32[24,256,1024]{2,1,0:T(8,128)} custom-call(f32[24,256,1024]{2,1,0:T(8,128)} %mom.3, bf16[24,256,1024]{2,1,0:T(8,128)(2,1)} %grad.3, bf16[8,256,1024]{2,1,0:T(8,128)(2,1)} %wave_2.1._), custom_call_target="tpu_custom_call" | custom-call | flops 629145600 | bytes 62914560 | tf_op jit(solution)/shard_map/momentum/pallas_call | solution.py:365
  573.5 0.0 all-gather.11.cloned.1.call-done
  573.5 43.1 %place_0.1.refs_0_ = bf16[24,2048,1024]{2,1,0:T(8,128)(2,1)} custom-call(bf16[8,8,256,1024]{3,2,1,0:T(8,128)(2,1)} %bitcast.3, f32[24,256,1024]{2,1,0:T(8,128)} %momentum.1.refs_0_), custom_call_target="tpu_custom_call" | custom-call | flops 671088640 | bytes 67108864 | tf_op jit(solution)/shard_map/place_0/pallas_call | solution.py:380
  616.5 0.0 all-gather.9.cloned.1.call-done
  616.5 43.1 %place_1.1.refs_0_ = bf16[24,2048,1024]{2,1,0:T(8,128)(2,1)} custom-call(bf16[8,8,256,1024]{3,2,1,0:T(8,128)(2,1)} %bitcast.4, bf16[24,2048,1024]{2,1,0:T(8,128)(2,1)} %place_0.1.refs_0_), custom_call_target="tpu_custom_call", output_to_operand_aliasing={{}: (1, {})} | custom-call | flops 671088640 | bytes 67108864 | tf_op jit(solution)/shard_map/place_1/pallas_call | solution.py:380
  659.6 95.8 %all-gather.7.cloned.1.call-done = bf16[64,256,1024]{2,1,0:T(8,128)(2,1)} async-done(((bf16[8,256,1024]{2,1,0:T(8,128)(2,1)}), bf16[64,256,1024]{2,1,0:T(8,128)(2,1)}) %all-gather.7.cloned.1.call-update) | async-done | bytes 33554448 | tf_op jit(solution)/shard_map/all_gather | solution.py:364
  755.5 43.1 %place_2.1 = bf16[24,2048,1024]{2,1,0:T(8,128)(2,1)} custom-call(bf16[8,8,256,1024]{3,2,1,0:T(8,128)(2,1)} %bitcast.5, bf16[24,2048,1024]{2,1,0:T(8,128)(2,1)} %place_1.1.refs_0_), custom_call_target="tpu_custom_call", output_to_operand_aliasing={{}: (1, {})} | custom-call | flops 671088640 | bytes 67108864 | tf_op jit(solution)/shard_map/place_2/pallas_call | solution.py:380
Async XLA Ops:
  7.2 566.3 %all-gather.11.cloned.1.call-start = ((), (), s32[]{:S(2)}) async-start(), calls=%async_computation.2 | async-start | bytes 37748736 | tf_op jit(solution)/shard_map/all_gather | solution.py:352
  200.6 415.9 %all-gather.9.cloned.1.call-start = ((), (), s32[]{:S(2)}) async-start(), calls=%async_computation.1 | async-start | bytes 37748736 | tf_op jit(solution)/shard_map/all_gather | solution.py:364
  373.3 382.1 %all-gather.7.cloned.1.call-start = ((), (), s32[]{:S(2)}) async-start(), calls=%async_computation | async-start | bytes 37748736 | tf_op jit(solution)/shard_map/all_gather | solution.py:364
Sparse Core Ops, SparseCore 0:
  200.7 199.2 all-gather.10
  401.6 198.5 all-gather.8
  601.8 153.5 all-gather.6

commit v2 on v1

--- a/solution.py
+++ b/solution.py
@@ -7,6 +7,7 @@
 from jax.experimental import pallas as pl
 from jax.experimental.pallas import tpu as pltpu
 from jax.sharding import PartitionSpec as P
+
 
 NS_ITERS = 5
 MOMENTUM = 0.95
@@ -21,7 +22,8 @@
 CORES = 2
 BLK = 256
 CHUNK = 32
-VMEM_LIMIT = 60 * 1024 * 1024
+SLOTS = 8
+VMEM_LIMIT = 67043328
 F32 = jnp.float32
 BF16 = jnp.bfloat16
 
@@ -92,13 +94,8 @@
     lax.fori_loop(0, group, load, 0)
 
 
-def orthogonalize_wave(me, wave, group, chips, land, norms, w_hbm, w_out, y, gram, poly, norm_v, x_land, w_vmem, o_vmem,
-                       y_sem, x_send, x_recv, w_sem, o_sem):
-    rows, cols = y.shape
-    rows_dev = rows // group
-    own_k = group - CORES
-    scale = 0.2 * math.sqrt(max(rows, cols))
-
+def iterate(wave, land, norms, y, gram, poly, norm_v, y_sem):
+    rows = y.shape[0]
     load_y = pltpu.make_async_copy(land.at[wave], y, y_sem.at[0])
     load_n = pltpu.make_async_copy(norms.at[wave], norm_v, y_sem.at[1])
     load_y.start()
@@ -115,6 +112,38 @@
 
     lax.fori_loop(0, rows // CHUNK, normalise, 0)
     newton_schulz(y, gram, poly)
+
+
+def new_rows(scale, w_vmem, x_vmem, o_vmem, k):
+    def chunk(i, c):
+        at = aligned(i * CHUNK, CHUNK)
+        w_old = w_vmem[k, at, :]
+        ortho = x_vmem[k, at, :].astype(F32) * scale
+        o_vmem[k, at, :] = (w_old - LEARN_RATE * (ortho + WEIGHT_DECAY * w_old)).astype(BF16)
+        return c
+
+    lax.fori_loop(0, w_vmem.shape[1] // CHUNK, chunk, 0)
+
+
+def store_rows(o_vmem, w_lo, w_hi, o_sem, k, owner, act):
+    half = w_lo.shape[0]
+
+    @pl.when(owner < half)
+    def _():
+        act(pltpu.make_async_copy(o_vmem.at[k], w_lo.at[owner], o_sem.at[k]))
+
+    @pl.when(owner >= half)
+    def _():
+        act(pltpu.make_async_copy(o_vmem.at[k], w_hi.at[owner - half], o_sem.at[k]))
+
+
+def orthogonalize_wave(me, wave, group, chips, land, norms, w_hbm, w_lo, w_hi, y, gram, poly, norm_v, x_land, w_vmem, o_vmem,
+                       y_sem, x_send, x_recv, w_sem, o_sem, then):
+    rows, cols = y.shape
+    rows_dev = rows // group
+    own_k = group - CORES
+    scale = 0.2 * math.sqrt(max(rows, cols))
+    iterate(wave, land, norms, y, gram, poly, norm_v, y_sem)
 
     def row_copy(k):
         target = target_of(me, k, chips)
@@ -130,6 +159,7 @@
     for k in range(group):
         if k != own_k:
             row_copy(k).start()
+    then()
     own = pltpu.make_async_copy(y.at[aligned(me * rows_dev, rows_dev)], x_land.at[own_k], y_sem.at[0])
     own.start()
 
@@ -146,22 +176,15 @@
         def _():
             row_copy(k).wait_recv()
 
-        def chunk(i, c2):
-            at = aligned(i * CHUNK, CHUNK)
-            w_old = w_vmem[k, at, :]
-            ortho = x_land[k, at, :].astype(F32) * scale
-            o_vmem[k, at, :] = (w_old - LEARN_RATE * (ortho + WEIGHT_DECAY * w_old)).astype(BF16)
-            return c2
-
-        lax.fori_loop(0, rows_dev // CHUNK, chunk, 0)
-        pltpu.make_async_copy(o_vmem.at[k], w_out.at[owner], o_sem.at[k]).start()
+        new_rows(scale, w_vmem, x_land, o_vmem, k)
+        store_rows(o_vmem, w_lo, w_hi, o_sem, k, owner, lambda copy: copy.start())
         return c
 
     lax.fori_loop(0, group, update, 0)
 
     def finish(k, c):
         owner = source_of(me, k, chips)
-        pltpu.make_async_copy(o_vmem.at[k], w_out.at[owner], o_sem.at[k]).wait()
+        store_rows(o_vmem, w_lo, w_hi, o_sem, k, owner, lambda copy: copy.wait())
 
         @pl.when(k != own_k)
         def _():
@@ -172,7 +195,7 @@
     lax.fori_loop(0, group, finish, 0)
 
 
-def first_kernel(group, waves, mom, grad, w_hbm, w_out, land, norms, send, norm_send, mom_v, grad_v, load_sem, m_send, m_recv,
+def first_kernel(group, waves, mom, grad, w_hbm, w_lo, w_hi, land, norms, send, norm_send, mom_v, grad_v, load_sem, m_send, m_recv,
                  n_send, n_recv, l_sem, *work):
     me = lax.axis_index("data")
     chips = group // CORES
@@ -180,11 +203,14 @@
     rows_dev, cols = mom.shape[1:]
     steps = waves * group
     greet_group(me, group, chips)
-    y, gram, poly, norm_v, x_land, w_vmem, o_vmem, y_sem, x_send, x_recv, w_sem, o_sem = work
+    _, _, _, _, _, w_vmem, _, _, _, _, w_sem, _ = work
     mine = aligned(me * rows_dev, rows_dev)
 
+    def block_of(t):
+        return t // group, lax.rem(lax.rem(t, group) * (group // 2 + 1), group)
+
     def loads(t):
-        wave, k = t // group, lax.rem(t, group)
+        wave, k = block_of(t)
         mat = wave * group + target_of(me, k, chips)
         slot = lax.rem(t, 2)
         return (
@@ -211,7 +237,7 @@
         )
 
     def dispatch(t):
-        wave, k = t // group, lax.rem(t, group)
+        wave, k = block_of(t)
 
         @pl.when(k == own_k)
         def _():
@@ -235,11 +261,13 @@
         for copy in loads(t):
             copy.wait()
         slot = lax.rem(t, 2)
+        wave, k = block_of(t)
+        at_send = wave * group + k
 
         def chunk(i, acc):
             at = aligned(i * CHUNK, CHUNK)
             new = MOMENTUM * mom_v[slot, at, :] + grad_v[slot, at, :].astype(F32)
-            send[t, at, :] = new.astype(BF16)
+            send[at_send, at, :] = new.astype(BF16)
             sq = new * new
             for r in range(0, CHUNK, 8):
                 acc = acc + sq[r:r + 8, :]
@@ -249,7 +277,7 @@
         part = acc[:, 0:128]
         for col in range(128, cols, 128):
             part = part + acc[:, col:col + 128]
-        norm_send[t] = part
+        norm_send[at_send] = part
 
         @pl.when(t > 0)
         def _():
@@ -258,7 +286,6 @@
         return c
 
     lax.fori_loop(0, steps, form, 0)
-    dispatch(jnp.int32(steps - 1))
     start_weights(me, 0, group, w_hbm, w_vmem, w_sem, chips)
 
     def arrived(wave):
@@ -270,7 +297,7 @@
             copy.wait()
 
     arrived(0)
-    orthogonalize_wave(me, 0, group, chips, land, norms, w_hbm, w_out, *work)
+    orthogonalize_wave(me, 0, group, chips, land, norms, w_hbm, w_lo, w_hi, *work, then=lambda: dispatch(jnp.int32(steps - 1)))
     for wave in range(1, waves):
         arrived(wave)
     for wave in range(waves):
@@ -280,27 +307,91 @@
                     copy.wait_send()
 
 
-def later_kernel(group, wave, land, norms, w_hbm, w_out, *work):
+def later_kernel(group, wave, land, norms, *refs):
     me = lax.axis_index("data")
     chips = group // CORES
-    greet_group(me, group, chips)
-    start_weights(me, wave, group, w_hbm, work[5], work[10], chips)
-    orthogonalize_wave(me, wave, group, chips, land, norms, w_hbm, w_out, *work)
+    outs, (y, gram, poly, norm_v, y_sem, o_sem) = refs[:group], refs[group:]
+    rows_dev = y.shape[0] // group
+    iterate(wave, land, norms, y, gram, poly, norm_v, y_sem)
+    stores = [
+        pltpu.make_async_copy(y.at[aligned(target_of(me, k, chips) * rows_dev, rows_dev)], outs[k], o_sem.at[k])
+        for k in range(group)
+    ]
+    for copy in stores:
+        copy.start()
+    for copy in stores:
+        copy.wait()
+
+
+def update_kernel(group, wave, scale, *refs):
+    me = lax.axis_index("data")
+    chips = group // CORES
+    blocks, (w_hbm, w_lo, w_hi, x_vmem, w_vmem, o_vmem, x_sem, w_sem, o_sem) = refs[:group], refs[group:]
+    owners = [source_of(me, k, chips) for k in range(group)]
+    loads = [
+        (
+            pltpu.make_async_copy(blocks[k], x_vmem.at[k], x_sem.at[k]),
+            pltpu.make_async_copy(w_hbm.at[wave * group + owners[k]], w_vmem.at[k], w_sem.at[k]),
+        )
+        for k in range(group)
+    ]
+    for pair in loads:
+        for copy in pair:
+            copy.start()
+    for k in range(group):
+        for copy in loads[k]:
+            copy.wait()
+        new_rows(scale, w_vmem, x_vmem, o_vmem, k)
+        store_rows(o_vmem, w_lo, w_hi, o_sem, k, owners[k], lambda copy: copy.start())
+    for k in range(group):
+        store_rows(o_vmem, w_lo, w_hi, o_sem, k, owners[k], lambda copy: copy.wait())
 
 
 def momentum_kernel(mom, grad, _, out):
     out[...] = MOMENTUM * mom[...] + grad[...].astype(F32)
 
 
-def place_kernel(src, *refs):
-    refs[-1][...] = src[0]
+def place_kernel(group, wave, pieces, *refs):
+    me = lax.axis_index("data")
+    chips = group // CORES
+    out, buf, in_sem, out_sem = refs[-4:]
+    slots, rows_dev = buf.shape[:2]
+    lag = slots // 2
+    steps = [(p, first, o, dx, dc) for p, (first, count, dx, dc) in enumerate(pieces) for o in range(count)]
+
+    def take(t):
+        p, _, o, _, _ = steps[t]
+        return pltpu.make_async_copy(refs[p].at[o], buf.at[t % slots], in_sem.at[t % slots])
+
+    def put(t):
+        _, first, o, dx, dc = steps[t]
+        owner_rows = lax.rem(me // CORES + chips - dx, chips) * CORES + lax.rem(lax.rem(me, CORES) + dc, CORES)
+        dst = out.at[wave * group + first + o, aligned(owner_rows * rows_dev, rows_dev)]
+        return pltpu.make_async_copy(buf.at[t % slots], dst, out_sem.at[t % slots])
+
+    for t in range(len(steps) + lag):
+        if t < len(steps):
+            if t >= slots:
+                put(t - slots).wait()
+            take(t).start()
+        if t >= lag:
+            take(t - lag).wait()
+            put(t - lag).start()
+    for t in range(max(len(steps) - slots, 0), len(steps)):
+        put(t).wait()
 
 
 def solution(mesh):
     group = mesh.shape["data"]
+    chips = group // CORES
+    half = group // 2
     row_spec = P("stage", "data", None)
     full_spec = P("stage", None, None)
     any_spec = pl.BlockSpec(memory_space=pl.ANY)
+
+    def shift(block, dx, dc):
+        pairs = [(d, (d // CORES + dx) % chips * CORES + (d % CORES + dc) % CORES) for d in range(group)]
+        return lax.ppermute(block, "data", pairs)
 
     def local_step(w_rows, mom_rows, grad_rows):
         mats, rows_dev, cols = mom_rows.shape
@@ -321,18 +412,40 @@
             pltpu.SemaphoreType.DMA((group,)),
             pltpu.SemaphoreType.DMA((group,)),
         ]
-        w_new_shape = jax.ShapeDtypeStruct((group, rows_dev, cols), BF16)
+        half_shape = jax.ShapeDtypeStruct((half, rows_dev, cols), BF16)
         cost = pl.CostEstimate(flops=ns_flops, bytes_accessed=8 * rows * cols, transcendentals=0)
-        w_new, land, norms = pl.pallas_call(
+
+        def place(params, wave, pieces, after=None):
+            blocks = [block for block, *_ in pieces]
+            count = len(blocks)
+            operands = blocks + [x for x in (params, after) if x is not None]
+            return pl.pallas_call(
+                functools.partial(place_kernel, group, wave, tuple(tuple(piece[1:]) for piece in pieces)),
+                out_shape=jax.ShapeDtypeStruct((mats, rows, cols), BF16),
+                in_specs=[any_spec] * len(operands),
+                out_specs=any_spec,
+                scratch_shapes=[
+                    pltpu.VMEM((SLOTS, rows_dev, cols), BF16),
+                    pltpu.SemaphoreType.DMA((SLOTS,)),
+                    pltpu.SemaphoreType.DMA((SLOTS,)),
+                ],
+                input_output_aliases={count: 0} if params is not None else {},
+                compiler_params=pltpu.CompilerParams(vmem_limit_bytes=VMEM_LIMIT),
+                cost_estimate=pl.CostEstimate(
+                    flops=count * half * rows_dev * cols * 40, bytes_accessed=4 * count * half * rows_dev * cols, transcendentals=0),
+            )(*operands)
+
+        w_lo, w_hi, land, norms = pl.pallas_call(
             functools.partial(first_kernel, group, waves),
             name="first_wave",
             out_shape=(
-                w_new_shape,
+                half_shape,
+                half_shape,
                 jax.ShapeDtypeStruct((waves, rows, cols), BF16),
                 jax.ShapeDtypeStruct((waves, group, 8, 128), F32),
             ),
             in_specs=[any_spec] * 3,
-            out_specs=(any_spec,) * 3,
+            out_specs=(any_spec,) * 4,
             scratch_shapes=[
                 pltpu.VMEM((mats, rows_dev, cols), BF16),
                 pltpu.VMEM((mats, 8, 128), F32),
@@ -349,19 +462,54 @@
             compiler_params=pltpu.CompilerParams(collective_id=0, has_side_effects=True, vmem_limit_bytes=VMEM_LIMIT),
             cost_estimate=cost,
         )(mom_rows, grad_rows, w_rows)
-        gathered = [lax.all_gather(w_new, "data", axis=0)]
+
+        def spread(lo, hi):
+            up_lo, down_hi = shift(lo, 1, 0), shift(hi, chips - 1, 0)
+            up_hi, down_lo = shift(hi, 1, 0), shift(lo, chips - 1, 0)
+            return up_lo, down_lo, up_hi, down_hi
+
+        def pass_on(near):
+            return shift(near[0], 1, 0), shift(near[3], chips - 1, 0)
+
+        def part_cores(block, first):
+            count = block.shape[0]
+            return (block, first, count, 2, 0), (shift(block, 0, 1), first, count, 2, 1)
+
+        def both_cores(pair, dx):
+            lo, hi = pair
+            return [(lo, 0, half, dx, 0), (hi, half, half, dx, 0)], [
+                (shift(lo, 0, 1), 0, half, dx, 1), (shift(hi, 0, 1), half, half, dx, 1)
+            ]
+
+        mom_after = w_lo
+        own, near, far = [(w_lo, w_hi)], [spread(w_lo, w_hi)], []
+        scale = 0.2 * math.sqrt(max(rows, cols))
         for wave in range(1, waves):
-            w_new = pl.pallas_call(
+            x_rows = pl.pallas_call(
                 functools.partial(later_kernel, group, wave),
-                name=f"wave_{wave}",
-                out_shape=w_new_shape,
-                in_specs=[any_spec] * 3,
-                out_specs=any_spec,
-                scratch_shapes=work,
-                compiler_params=pltpu.CompilerParams(collective_id=wave, has_side_effects=True, vmem_limit_bytes=VMEM_LIMIT),
+                out_shape=(jax.ShapeDtypeStruct((rows_dev, cols), BF16),) * group,
+                in_specs=[any_spec] * 2,
+                out_specs=(any_spec,) * group,
+                scratch_shapes=work[:4] + [pltpu.SemaphoreType.DMA((2,)), pltpu.SemaphoreType.DMA((group,))],
+                compiler_params=pltpu.CompilerParams(vmem_limit_bytes=VMEM_LIMIT),
                 cost_estimate=cost,
-            )(land, norms, w_rows)
-            gathered.append(lax.all_gather(w_new, "data", axis=0))
+            )(land, norms)
+            x_rows = [
+                x_rows[k] if k == group - CORES else shift(x_rows[k], (k // CORES + 1) % chips, k % CORES)
+                for k in range(group)
+            ]
+            w_lo, w_hi = pl.pallas_call(
+                functools.partial(update_kernel, group, wave, scale),
+                out_shape=(half_shape, half_shape),
+                in_specs=[any_spec] * (group + 1),
+                out_specs=(any_spec,) * 2,
+                scratch_shapes=work[4:7] + [pltpu.SemaphoreType.DMA((group,))] * 3,
+                compiler_params=pltpu.CompilerParams(vmem_limit_bytes=VMEM_LIMIT),
+                cost_estimate=pl.CostEstimate(flops=rows * cols * 400, bytes_accessed=8 * rows * cols, transcendentals=0),
+            )(*x_rows, w_rows)
+            far.append(pass_on(near[-1]))
+            own.append((w_lo, w_hi))
+            near.append(spread(w_lo, w_hi))
         mom_new = pl.pallas_call(
             momentum_kernel,
             name="momentum",
@@ -373,20 +521,33 @@
                 any_spec,
             ],
             out_specs=pl.BlockSpec((1, rows_dev, cols), lambda i: (i, 0, 0)),
+            compiler_params=pltpu.CompilerParams(vmem_limit_bytes=VMEM_LIMIT),
             cost_estimate=pl.CostEstimate(flops=mats * rows_dev * cols * 100, bytes_accessed=10 * mats * rows_dev * cols, transcendentals=0),
-        )(mom_rows, grad_rows, w_new)
-        params = mom_new
-        for wave in range(waves):
-            params = pl.pallas_call(
-                place_kernel,
-                name=f"place_{wave}",
-                grid=(group, group),
-                out_shape=jax.ShapeDtypeStruct((mats, rows, cols), BF16),
-                in_specs=[pl.BlockSpec((1, 1, rows_dev, cols), lambda o, d: (d, o, 0, 0)), any_spec],
-                out_specs=pl.BlockSpec((1, rows_dev, cols), lambda o, d, wave=wave: (wave * group + o, d, 0)),
-                input_output_aliases={1: 0} if wave else {},
-                cost_estimate=pl.CostEstimate(flops=group * rows * cols * 40, bytes_accessed=4 * group * rows * cols, transcendentals=0),
-            )(gathered[wave], params)
+        )(mom_rows, grad_rows, mom_after)
+
+        own_p = [both_cores(own[w], 0) for w in range(waves)]
+        up_p = [both_cores(near[w][0::2], 1) for w in range(waves)]
+        down_p = [both_cores(near[w][1::2], chips - 1) for w in range(waves)]
+        far_p = [both_cores(far[w], 2) for w in range(waves - 1)]
+        last = waves - 1
+        params = None
+        for w in range(last):
+            params = place(params, w, sum(own_p[w], []))
+            params = place(params, w, sum(up_p[w] + down_p[w], []))
+            if w < last - 1:
+                params = place(params, w, sum(far_p[w], []))
+        params = place(params, last, sum(own_p[last], []))
+        params = place(params, last - 1, sum(far_p[last - 1], []))
+        params = place(params, last, sum(up_p[last] + down_p[last], []))
+        first_part, last_part = [], []
+        for block, dx, first in ((near[last][0], 1, 0), (near[last][3], chips - 1, half)):
+            cut = half - 1
+            for rows_of, at, part in ((block[:cut], first, first_part), (block[cut:], first + cut, last_part)):
+                far_block = shift(rows_of, dx, 0)
+                part.append(part_cores(far_block, at))
+        params = place(params, last, [p for pair in first_part for p in pair])
+        params = place(params, last, [pair[0] for pair in last_part])
+        params = place(params, last, [pair[1] for pair in last_part])
         return params, mom_new
 
     return jax.shard_map(local_step, mesh=mesh, in_specs=(row_spec,) * 3, out_specs=(full_spec, row_spec), check_vma=False)

time: 809 us -> 989 us (1.22)
  waiting for transfers between devices: 96 us -> 461 us
  Pallas kernels: 695 us -> 464 us
  starting transfers between devices: 0.19 us -> 58.4 us
  between operations: 13.8 us -> 1.2 us
    ppermute x0 -> x60, waiting for transfers between devices: none -> 461 us  [shift(): return lax.ppermute(block, 'data', pairs)]
    pallas_call x5 -> x15, Pallas kernels: 474 us -> 244 us  [the longest x2 150 us: local_step(): pl.pallas_call(functools.partial(later_kernel, group, wave), out_shape=(j...]
    all_gather x3 -> x0, waiting for transfers between devices: 95.8 us -> none  [the longest x2 95.8 us: local_step(): gathered.append(lax.all_gather(w_new, 'data', axis=0))]
    ppermute x0 -> x60, starting transfers between devices: none -> 58.4 us  [shift(): return lax.ppermute(block, 'data', pairs)]
  transfers between devices with their start and end apart: 3 -> 60, of which waited for: 1 -> 29; matrix products, arithmetic and copies ran while one was open for 0% -> 0% of each run, Pallas kernels for 57% -> 20%
where the time goes in v2:
time: 989 us; the launch traced here: 987 us
  Pallas kernels  464 us (47%)
  waiting for transfers between devices  461 us (47%)
  starting transfers between devices  58.4 us (6%)
    ppermute x60, waiting for transfers between devices, shift(): return lax.ppermute(block, 'data', pairs)  461 us
    pallas_call x1, Pallas kernels, local_step(): pl.pallas_call(functools.partial(first_kernel, group, waves), name='first...  191 us
    pallas_call x2, Pallas kernels, local_step(): pl.pallas_call(functools.partial(later_kernel, group, wave), out_shape=(j...  150 us
    pallas_call x11, Pallas kernels, place(): pl.pallas_call(functools.partial(place_kernel, group, wave, tuple((tuple(...  80.4 us
    ppermute x60, starting transfers between devices, shift(): return lax.ppermute(block, 'data', pairs)  58.4 us
    pallas_call x1, Pallas kernels, local_step(): pl.pallas_call(momentum_kernel, name='momentum', grid=(mats,), out_shape=...  28.2 us
  transfers between devices with their start and end apart: 60, of which 29 were waited for; matrix products, arithmetic and copies ran while one was open for 0% of the time, Pallas kernels for 20%

profile of v2, /device:TPU:113, one launch (start us, length us, event | category | flops | bytes accessed | tf_op | source)
XLA Modules:
  0.0 986.7 jit_solution(9499479919322671829)
XLA Ops:
  0.6 191.0 %first_wave.1 = (bf16[4,256,1024]{2,1,0:T(8,128)(2,1)}, bf16[4,256,1024]{2,1,0:T(8,128)(2,1)}, bf16[3,2048,1024]{2,1,0:T(8,128)(2,1)}, f32[3,8,8,128]{3,2,1,0:T(8,128)}) custom-call(f32[24,256,1024]{2,1,0:T(8,128)} %mom.3, bf16[24,256,1024]{2,1,0:T(8,128)(2,1)} %grad.3, f32[24,256,1024]{2,1,0:T(8,128)} %refs_8_.3), custom_call_target="tpu_custom_call" | custom-call | flops 53687091200 | bytes 16777216 | tf_op jit(solution)/shard_map/first_wave/pallas_call | solution.py:438
  191.7 75.0 %shard_map.52 = (bf16[256,1024]{1,0:T(8,128)(2,1)}, bf16[256,1024]{1,0:T(8,128)(2,1)}, bf16[256,1024]{1,0:T(8,128)(2,1)}, bf16[256,1024]{1,0:T(8,128)(2,1)}, bf1...) custom-call(bf16[3,2048,1024]{2,1,0:T(8,128)(2,1)} %get-tuple-element, ...), custom_call_target="tpu_custom_call" | custom-call | flops 53687091200 | bytes 16777216 | tf_op jit(solution)/shard_map/pallas_call | solution.py:488
  274.4 7.8 collective-permute-done.23.refs_0_
  284.9 8.6 collective-permute-done.24.refs_1_
  293.8 75.0 %shard_map.50 = (bf16[256,1024]{1,0:T(8,128)(2,1)}, bf16[256,1024]{1,0:T(8,128)(2,1)}, bf16[256,1024]{1,0:T(8,128)(2,1)}, bf16[256,1024]{1,0:T(8,128)(2,1)}, bf1...) custom-call(bf16[3,2048,1024]{2,1,0:T(8,128)(2,1)} %get-tuple-element, ...), custom_call_target="tpu_custom_call" | custom-call | flops 53687091200 | bytes 16777216 | tf_op jit(solution)/shard_map/pallas_call | solution.py:488
  373.7 10.2 %collective-permute-done.refs_0_ = bf16[256,1024]{1,0:T(8,128)(2,1)} collective-permute-done((bf16[256,1024]{1,0:T(8,128)(2,1)}, bf16[256,1024]{1,0:T(8,128)(2,1)}, u32[]{:S(2)}, u32[]{:S(2)}) %collective-permute-start) | collective-permute-done | bytes 524320 | tf_op jit(solution)/shard_map/ppermute | solution.py:394
  385.5 10.4 %collective-permute-done.1.refs_1_ = bf16[256,1024]{1,0:T(8,128)(2,1)} collective-permute-done((bf16[256,1024]{1,0:T(8,128)(2,1)}, bf16[256,1024]{1,0:T(8,128)(2,1)}, u32[]{:S(2)}, u32[]{:S(2)}) %collective-permute-start.1) | collective-permute-done | bytes 524320 | tf_op jit(solution)/shard_map/ppermute | solution.py:394
  395.9 10.6 %collective-permute-done.2.refs_2_ = bf16[256,1024]{1,0:T(8,128)(2,1)} collective-permute-done((bf16[256,1024]{1,0:T(8,128)(2,1)}, bf16[256,1024]{1,0:T(8,128)(2,1)}, u32[]{:S(2)}, u32[]{:S(2)}) %collective-permute-start.2) | collective-permute-done | bytes 524320 | tf_op jit(solution)/shard_map/ppermute | solution.py:394
  406.5 12.9 %collective-permute-done.3.refs_3_ = bf16[256,1024]{1,0:T(8,128)(2,1)} collective-permute-done((bf16[256,1024]{1,0:T(8,128)(2,1)}, bf16[256,1024]{1,0:T(8,128)(2,1)}, u32[]{:S(2)}, u32[]{:S(2)}) %collective-permute-start.3) | collective-permute-done | bytes 524320 | tf_op jit(solution)/shard_map/ppermute | solution.py:394
  419.5 14.7 %collective-permute-done.5.refs_5_ = bf16[256,1024]{1,0:T(8,128)(2,1)} collective-permute-done((bf16[256,1024]{1,0:T(8,128)(2,1)}, bf16[256,1024]{1,0:T(8,128)(2,1)}, u32[]{:S(2)}, u32[]{:S(2)}) %collective-permute-start.5) | collective-permute-done | bytes 524320 | tf_op jit(solution)/shard_map/ppermute | solution.py:394
  445.6 18.0 %collective-permute-done.46.refs_0_ = bf16[4,256,1024]{2,1,0:T(8,128)(2,1)} collective-permute-done((bf16[4,256,1024]{2,1,0:T(8,128)(2,1)}, bf16[4,256,1024]{2,1,0:T(8,128)(2,1)}, u32[]{:S(2)}, u32[]{:S(2)}) %collective-permute-start.46) | collective-permute-done | bytes 2097184 | tf_op jit(solution)/shard_map/ppermute | solution.py:394
  464.0 12.4 %collective-permute-done.55.refs_4_ = bf16[4,256,1024]{2,1,0:T(8,128)(2,1)} collective-permute-done((bf16[4,256,1024]{2,1,0:T(8,128)(2,1)}, bf16[4,256,1024]{2,1,0:T(8,128)(2,1)}, u32[]{:S(2)}, u32[]{:S(2)}) %collective-permute-start.55) | collective-permute-done | bytes 2097184 | tf_op jit(solution)/shard_map/ppermute | solution.py:394
  477.0 43.3 %collective-permute-done.48.refs_5_ = bf16[4,256,1024]{2,1,0:T(8,128)(2,1)} collective-permute-done((bf16[4,256,1024]{2,1,0:T(8,128)(2,1)}, bf16[4,256,1024]{2,1,0:T(8,128)(2,1)}, u32[]{:S(2)}, u32[]{:S(2)}) %collective-permute-start.48) | collective-permute-done | bytes 2097184 | tf_op jit(solution)/shard_map/ppermute | solution.py:394
  526.1 7.0 shard_map.51
  533.7 19.8 %collective-permute-done.30.refs_0_ = bf16[4,256,1024]{2,1,0:T(8,128)(2,1)} collective-permute-done((bf16[4,256,1024]{2,1,0:T(8,128)(2,1)}, bf16[4,256,1024]{2,1,0:T(8,128)(2,1)}, u32[]{:S(2)}, u32[]{:S(2)}) %collective-permute-start.30) | collective-permute-done | bytes 2097184 | tf_op jit(solution)/shard_map/ppermute | solution.py:394
  553.9 15.2 %collective-permute-done.32.refs_5_ = bf16[4,256,1024]{2,1,0:T(8,128)(2,1)} collective-permute-done((bf16[4,256,1024]{2,1,0:T(8,128)(2,1)}, bf16[4,256,1024]{2,1,0:T(8,128)(2,1)}, u32[]{:S(2)}, u32[]{:S(2)}) %collective-permute-start.32) | collective-permute-done | bytes 2097184 | tf_op jit(solution)/shard_map/ppermute | solution.py:394
  569.1 29.3 %collective-permute-done.38.refs_1_ = bf16[4,256,1024]{2,1,0:T(8,128)(2,1)} collective-permute-done((bf16[4,256,1024]{2,1,0:T(8,128)(2,1)}, bf16[4,256,1024]{2,1,0:T(8,128)(2,1)}, u32[]{:S(2)}, u32[]{:S(2)}) %collective-permute-start.38) | collective-permute-done | bytes 2097184 | tf_op jit(solution)/shard_map/ppermute | solution.py:394
  598.4 15.6 %collective-permute-done.41.refs_4_ = bf16[4,256,1024]{2,1,0:T(8,128)(2,1)} collective-permute-done((bf16[4,256,1024]{2,1,0:T(8,128)(2,1)}, bf16[4,256,1024]{2,1,0:T(8,128)(2,1)}, u32[]{:S(2)}, u32[]{:S(2)}) %collective-permute-start.41) | collective-permute-done | bytes 2097184 | tf_op jit(solution)/shard_map/ppermute | solution.py:394
  619.6 23.6 %collective-permute-done.7.refs_0_ = bf16[4,256,1024]{2,1,0:T(8,128)(2,1)S(1)} collective-permute-done((bf16[4,256,1024]{2,1,0:T(8,128)(2,1)}, bf16[4,256,1024]{2,1,0:T(8,128)(2,1)S(1)}, u32[]{:S(2)}, u32[]{:S(2)}) %collective-permute-start.7) | collective-permute-done | bytes 2097184 | tf_op jit(solution)/shard_map/ppermute | solution.py:394
  643.7 15.3 %collective-permute-done.10.refs_5_ = bf16[4,256,1024]{2,1,0:T(8,128)(2,1)S(1)} collective-permute-done((bf16[4,256,1024]{2,1,0:T(8,128)(2,1)}, bf16[4,256,1024]{2,1,0:T(8,128)(2,1)S(1)}, u32[]{:S(2)}, u32[]{:S(2)}) %collective-permute-start.10) | collective-permute-done | bytes 2097184 | tf_op jit(solution)/shard_map/ppermute | solution.py:394
  661.3 26.9 %collective-permute-done.17.refs_1_ = bf16[4,256,1024]{2,1,0:T(8,128)(2,1)S(1)} collective-permute-done((bf16[4,256,1024]{2,1,0:T(8,128)(2,1)}, bf16[4,256,1024]{2,1,0:T(8,128)(2,1)S(1)}, u32[]{:S(2)}, u32[]{:S(2)}) %collective-permute-start.17) | collective-permute-done | bytes 2097184 | tf_op jit(solution)/shard_map/ppermute | solution.py:394
  688.2 15.7 %collective-permute-done.20.refs_4_ = bf16[4,256,1024]{2,1,0:T(8,128)(2,1)} collective-permute-done((bf16[4,256,1024]{2,1,0:T(8,128)(2,1)}, bf16[4,256,1024]{2,1,0:T(8,128)(2,1)}, u32[]{:S(2)}, u32[]{:S(2)}) %collective-permute-start.20) | collective-permute-done | bytes 2097184 | tf_op jit(solution)/shard_map/ppermute | solution.py:394
  706.3 8.7 collective-permute-done.11.refs_1_
  715.1 15.3 %collective-permute-done.8.refs_0_ = bf16[1,256,1024]{2,1,0:T(8,128)(2,1)} collective-permute-done((bf16[1,256,1024]{2,1,0:T(8,128)(2,1)S(1)}, bf16[1,256,1024]{2,1,0:T(8,128)(2,1)}, u32[]{:S(2)}, u32[]{:S(2)}) %collective-permute-start.8) | collective-permute-done | bytes 524320 | tf_op jit(solution)/shard_map/ppermute | solution.py:394
  738.2 39.8 %collective-permute-done.47.refs_0_ = bf16[4,256,1024]{2,1,0:T(8,128)(2,1)S(1)} collective-permute-done((bf16[4,256,1024]{2,1,0:T(8,128)(2,1)}, bf16[4,256,1024]{2,1,0:T(8,128)(2,1)S(1)}, u32[]{:S(2)}, u32[]{:S(2)}) %collective-permute-start.47) | collective-permute-done | bytes 2097184 | tf_op jit(solution)/shard_map/ppermute | solution.py:394
  781.5 30.2 %collective-permute-done.13.refs_0_ = bf16[3,256,1024]{2,1,0:T(8,128)(2,1)} collective-permute-done((bf16[3,256,1024]{2,1,0:T(8,128)(2,1)S(1)}, bf16[3,256,1024]{2,1,0:T(8,128)(2,1)}, u32[]{:S(2)}, u32[]{:S(2)}) %collective-permute-start.13) | collective-permute-done | bytes 1572896 | tf_op jit(solution)/shard_map/ppermute | solution.py:394
  819.0 43.3 %collective-permute-done.31.refs_0_ = bf16[4,256,1024]{2,1,0:T(8,128)(2,1)S(1)} collective-permute-done((bf16[4,256,1024]{2,1,0:T(8,128)(2,1)}, bf16[4,256,1024]{2,1,0:T(8,128)(2,1)S(1)}, u32[]{:S(2)}, u32[]{:S(2)}) %collective-permute-start.31) | collective-permute-done | bytes 2097184 | tf_op jit(solution)/shard_map/ppermute | solution.py:394
  877.7 28.2 %momentum.1 = f32[24,256,1024]{2,1,0:T(8,128)} custom-call(f32[24,256,1024]{2,1,0:T(8,128)} %mom.3, bf16[24,256,1024]{2,1,0:T(8,128)(2,1)} %grad.3, bf16[4,256,1024]{2,1,0:T(8,128)(2,1)} %get-tuple-element.48.refs_0_._), custom_call_target="tpu_custom_call" | custom-call | flops 629145600 | bytes 62914560 | tf_op jit(solution)/shard_map/momentum/pallas_call | solution.py:513
  912.8 12.1 %shard_map.55.refs_4_ = bf16[24,2048,1024]{2,1,0:T(8,128)(2,1)} custom-call(bf16[4,256,1024]{2,1,0:T(8,128)(2,1)} %collective-permute-done.46.refs_0_, bf16[4,256,1024]{2,1,0:T(8,128)(2,1)} %collective-permute-done.52.refs_1_, bf16[4,256,1024]{2,1,0:T(8,128)(2,1)} %collective-permute-done.53.refs_2_, ...), custom_call_target="tpu_custom_call", output_to_operand_aliasing={{}: (8, {})} | custom-call | flops 335544320 | bytes 33554432 | tf_op jit(solution)/shard_map/pallas_call | solution.py:422
  924.9 6.9 shard_map.56.refs_4_
  938.7 12.1 %shard_map.58.refs_4_ = bf16[24,2048,1024]{2,1,0:T(8,128)(2,1)} custom-call(bf16[4,256,1024]{2,1,0:T(8,128)(2,1)} %collective-permute-done.30.refs_0_, bf16[4,256,1024]{2,1,0:T(8,128)(2,1)} %collective-permute-done.38.refs_1_, bf16[4,256,1024]{2,1,0:T(8,128)(2,1)} %copy-done.16, bf16[4,256,1024]{2,1,0:T(8,128)(2,1)} %copy-done.18, ...), custom_call_target="tpu_custom_call", output_to_operand_aliasing={{}: (8, {})} | custom-call | flops 335544320 | bytes 33554432 | tf_op jit(solution)/shard_map/pallas_call | solution.py:422
  964.6 12.1 %shard_map.61.refs_4_ = bf16[24,2048,1024]{2,1,0:T(8,128)(2,1)} custom-call(bf16[4,256,1024]{2,1,0:T(8,128)(2,1)} %copy-done, bf16[4,256,1024]{2,1,0:T(8,128)(2,1)} %copy-done.12, bf16[4,256,1024]{2,1,0:T(8,128)(2,1)} %copy-done.20, bf16[4,256,1024]{2,1,0:T(8,128)(2,1)} %copy-done.22, ...), custom_call_target="tpu_custom_call", output_to_operand_aliasing={{}: (8, {})} | custom-call | flops 335544320 | bytes 33554432 | tf_op jit(solution)/shard_map/pallas_call | solution.py:422
  (155 shorter events, 118.6 us)
Async XLA Ops:
  268.6 100.3 %collective-permute-start.25 = (bf16[256,1024]{1,0:T(8,128)(2,1)}, bf16[256,1024]{1,0:T(8,128)(2,1)}, u32[]{:S(2)}, u32[]{:S(2)}) collective-permute-start(bf16[256,1024]{1,0:T(8,128)(2,1)} %get-tuple-element.40), channel_id=1, source_target_pairs={{0,4},{1,5},{2,6},{3,7},{4,0},{5,1},{6,2},{7,3},{8,12},{9,13},{10,... | collective-permute-start | bytes 1572872 | tf_op jit(solution)/shard_map/ppermute | solution.py:394
  271.1 98.4 %collective-permute-start.26 = (bf16[256,1024]{1,0:T(8,128)(2,1)}, bf16[256,1024]{1,0:T(8,128)(2,1)}, u32[]{:S(2)}, u32[]{:S(2)}) collective-permute-start(bf16[256,1024]{1,0:T(8,128)(2,1)} %get-tuple-element.41), channel_id=1, source_target_pairs={{0,5},{1,4},{2,7},{3,6},{4,1},{5,0},{6,3},{7,2},{8,13},{9,12},{10,... | collective-permute-start | bytes 1572872 | tf_op jit(solution)/shard_map/ppermute | solution.py:394
  271.8 98.4 %collective-permute-start.27 = (bf16[256,1024]{1,0:T(8,128)(2,1)}, bf16[256,1024]{1,0:T(8,128)(2,1)}, u32[]{:S(2)}, u32[]{:S(2)}) collective-permute-start(bf16[256,1024]{1,0:T(8,128)(2,1)} %get-tuple-element.42), channel_id=1, source_target_pairs={{0,6},{1,7},{2,0},{3,1},{4,2},{5,3},{6,4},{7,5},{8,14},{9,15},{10,... | collective-permute-start | bytes 1572872 | tf_op jit(solution)/shard_map/ppermute | solution.py:394
  282.2 88.2 %collective-permute-start.28 = (bf16[256,1024]{1,0:T(8,128)(2,1)}, bf16[256,1024]{1,0:T(8,128)(2,1)}, u32[]{:S(2)}, u32[]{:S(2)}) collective-permute-start(bf16[256,1024]{1,0:T(8,128)(2,1)} %get-tuple-element.43), channel_id=1, source_target_pairs={{0,7},{1,6},{2,1},{3,0},{4,3},{5,2},{6,5},{7,4},{8,15},{9,14},{10,... | collective-permute-start | bytes 1572872 | tf_op jit(solution)/shard_map/ppermute | solution.py:394
  293.5 77.2 %collective-permute-start.29 = (bf16[256,1024]{1,0:T(8,128)(2,1)}, bf16[256,1024]{1,0:T(8,128)(2,1)}, u32[]{:S(2)}, u32[]{:S(2)}) collective-permute-start(bf16[256,1024]{1,0:T(8,128)(2,1)} %get-tuple-element.45), channel_id=1, source_target_pairs={{0,1},{1,0},{2,3},{3,2},{4,5},{5,4},{6,7},{7,6},{8,9},{9,8},{10,11... | collective-permute-start | bytes 1572872 | tf_op jit(solution)/shard_map/ppermute | solution.py:394
  369.4 67.7 %collective-permute-start.58 = (bf16[4,256,1024]{2,1,0:T(8,128)(2,1)}, bf16[4,256,1024]{2,1,0:T(8,128)(2,1)}, u32[]{:S(2)}, u32[]{:S(2)}) collective-permute-start(bf16[4,256,1024]{2,1,0:T(8,128)(2,1)} %get-tuple-element.48.refs_0_._), channel_id=1, source_target_pairs={{0,1},{1,0},{2,3},{3,2},{4,5},{5,4},{6,7},{7,6},{8,9},{9,8},{10,11... | collective-permute-start | bytes 6291464 | tf_op jit(solution)/shard_map/ppermute | solution.py:394
  370.4 74.3 %collective-permute-start.59 = (bf16[4,256,1024]{2,1,0:T(8,128)(2,1)}, bf16[4,256,1024]{2,1,0:T(8,128)(2,1)}, u32[]{:S(2)}, u32[]{:S(2)}) collective-permute-start(bf16[4,256,1024]{2,1,0:T(8,128)(2,1)} %get-tuple-element.49.refs_1_), channel_id=1, source_target_pairs={{0,1},{1,0},{2,3},{3,2},{4,5},{5,4},{6,7},{7,6},{8,9},{9,8},{10,11... | collective-permute-start | bytes 6291464 | tf_op jit(solution)/shard_map/ppermute | solution.py:394
  395.9 67.7 %collective-permute-start.46 = (bf16[4,256,1024]{2,1,0:T(8,128)(2,1)}, bf16[4,256,1024]{2,1,0:T(8,128)(2,1)}, u32[]{:S(2)}, u32[]{:S(2)}) collective-permute-start(bf16[4,256,1024]{2,1,0:T(8,128)(2,1)} %get-tuple-element.48.refs_0_._), channel_id=1, source_target_pairs={{0,2},{1,3},{2,4},{3,5},{4,6},{5,7},{6,0},{7,1},{8,10},{9,11},{10,... | collective-permute-start | bytes 6291464 | tf_op jit(solution)/shard_map/ppermute | solution.py:394
  436.5 83.8 %collective-permute-start.48 = (bf16[4,256,1024]{2,1,0:T(8,128)(2,1)}, bf16[4,256,1024]{2,1,0:T(8,128)(2,1)}, u32[]{:S(2)}, u32[]{:S(2)}) collective-permute-start(bf16[4,256,1024]{2,1,0:T(8,128)(2,1)} %get-tuple-element.49.refs_1_), channel_id=1, source_target_pairs={{0,6},{1,7},{2,0},{3,1},{4,2},{5,3},{6,4},{7,5},{8,14},{9,15},{10,... | collective-permute-start | bytes 6291464 | tf_op jit(solution)/shard_map/ppermute | solution.py:394
  437.1 86.3 %collective-permute-start.52 = (bf16[4,256,1024]{2,1,0:T(8,128)(2,1)}, bf16[4,256,1024]{2,1,0:T(8,128)(2,1)}, u32[]{:S(2)}, u32[]{:S(2)}) collective-permute-start(bf16[4,256,1024]{2,1,0:T(8,128)(2,1)} %get-tuple-element.49.refs_1_), channel_id=1, source_target_pairs={{0,2},{1,3},{2,4},{3,5},{4,6},{5,7},{6,0},{7,1},{8,10},{9,11},{10,... | collective-permute-start | bytes 6291464 | tf_op jit(solution)/shard_map/ppermute | solution.py:394
  444.8 78.7 %collective-permute-start.44 = (bf16[4,256,1024]{2,1,0:T(8,128)(2,1)}, bf16[4,256,1024]{2,1,0:T(8,128)(2,1)}, u32[]{:S(2)}, u32[]{:S(2)}) collective-permute-start(bf16[4,256,1024]{2,1,0:T(8,128)(2,1)} %get-tuple-element.46.refs_0_), channel_id=1, source_target_pairs={{0,1},{1,0},{2,3},{3,2},{4,5},{5,4},{6,7},{7,6},{8,9},{9,8},{10,11... | collective-permute-start | bytes 6291464 | tf_op jit(solution)/shard_map/ppermute | solution.py:394
  463.6 69.5 %collective-permute-start.45 = (bf16[4,256,1024]{2,1,0:T(8,128)(2,1)}, bf16[4,256,1024]{2,1,0:T(8,128)(2,1)}, u32[]{:S(2)}, u32[]{:S(2)}) collective-permute-start(bf16[4,256,1024]{2,1,0:T(8,128)(2,1)} %get-tuple-element.47.refs_1_), channel_id=1, source_target_pairs={{0,1},{1,0},{2,3},{3,2},{4,5},{5,4},{6,7},{7,6},{8,9},{9,8},{10,11... | collective-permute-start | bytes 6291464 | tf_op jit(solution)/shard_map/ppermute | solution.py:394
  476.4 77.1 %collective-permute-start.30 = (bf16[4,256,1024]{2,1,0:T(8,128)(2,1)}, bf16[4,256,1024]{2,1,0:T(8,128)(2,1)}, u32[]{:S(2)}, u32[]{:S(2)}) collective-permute-start(bf16[4,256,1024]{2,1,0:T(8,128)(2,1)} %get-tuple-element.46.refs_0_), channel_id=1, source_target_pairs={{0,2},{1,3},{2,4},{3,5},{4,6},{5,7},{6,0},{7,1},{8,10},{9,11},{10,... | collective-permute-start | bytes 6291464 | tf_op jit(solution)/shard_map/ppermute | solution.py:394
  523.4 75.0 %collective-permute-start.38 = (bf16[4,256,1024]{2,1,0:T(8,128)(2,1)}, bf16[4,256,1024]{2,1,0:T(8,128)(2,1)}, u32[]{:S(2)}, u32[]{:S(2)}) collective-permute-start(bf16[4,256,1024]{2,1,0:T(8,128)(2,1)} %get-tuple-element.47.refs_1_), channel_id=1, source_target_pairs={{0,2},{1,3},{2,4},{3,5},{4,6},{5,7},{6,0},{7,1},{8,10},{9,11},{10,... | collective-permute-start | bytes 6291464 | tf_op jit(solution)/shard_map/ppermute | solution.py:394
  523.4 90.6 %collective-permute-start.41 = (bf16[4,256,1024]{2,1,0:T(8,128)(2,1)}, bf16[4,256,1024]{2,1,0:T(8,128)(2,1)}, u32[]{:S(2)}, u32[]{:S(2)}) collective-permute-start(bf16[4,256,1024]{2,1,0:T(8,128)(2,1)} %get-tuple-element.46.refs_0_), channel_id=1, source_target_pairs={{0,6},{1,7},{2,0},{3,1},{4,2},{5,3},{6,4},{7,5},{8,14},{9,15},{10,... | collective-permute-start | bytes 6291464 | tf_op jit(solution)/shard_map/ppermute | solution.py:394
  533.1 80.9 %collective-permute-start.36 = (bf16[4,256,1024]{2,1,0:T(8,128)(2,1)}, bf16[4,256,1024]{2,1,0:T(8,128)(2,1)S(1)}, u32[]{:S(2)}, u32[]{:S(2)}) collective-permute-start(bf16[4,256,1024]{2,1,0:T(8,128)(2,1)} %get-tuple-element.36.refs_0_), channel_id=1, source_target_pairs={{0,1},{1,0},{2,3},{3,2},{4,5},{5,4},{6,7},{7,6},{8,9},{9,8},{10,11... | collective-permute-start | bytes 6291464 | tf_op jit(solution)/shard_map/ppermute | solution.py:394
  553.5 64.0 %collective-permute-start.37 = (bf16[4,256,1024]{2,1,0:T(8,128)(2,1)}, bf16[4,256,1024]{2,1,0:T(8,128)(2,1)S(1)}, u32[]{:S(2)}, u32[]{:S(2)}) collective-permute-start(bf16[4,256,1024]{2,1,0:T(8,128)(2,1)} %get-tuple-element.37.refs_1_), channel_id=1, source_target_pairs={{0,1},{1,0},{2,3},{3,2},{4,5},{5,4},{6,7},{7,6},{8,9},{9,8},{10,11... | collective-permute-start | bytes 6291464 | tf_op jit(solution)/shard_map/ppermute | solution.py:394
  569.1 74.2 %collective-permute-start.7 = (bf16[4,256,1024]{2,1,0:T(8,128)(2,1)}, bf16[4,256,1024]{2,1,0:T(8,128)(2,1)S(1)}, u32[]{:S(2)}, u32[]{:S(2)}) collective-permute-start(bf16[4,256,1024]{2,1,0:T(8,128)(2,1)} %get-tuple-element.36.refs_0_), channel_id=1, source_target_pairs={{0,2},{1,3},{2,4},{3,5},{4,6},{5,7},{6,0},{7,1},{8,10},{9,11},{10,... | collective-permute-start | bytes 6291464 | tf_op jit(solution)/shard_map/ppermute | solution.py:394
  598.4 60.5 %collective-permute-start.10 = (bf16[4,256,1024]{2,1,0:T(8,128)(2,1)}, bf16[4,256,1024]{2,1,0:T(8,128)(2,1)S(1)}, u32[]{:S(2)}, u32[]{:S(2)}) collective-permute-start(bf16[4,256,1024]{2,1,0:T(8,128)(2,1)} %get-tuple-element.37.refs_1_), channel_id=1, source_target_pairs={{0,6},{1,7},{2,0},{3,1},{4,2},{5,3},{6,4},{7,5},{8,14},{9,15},{10,... | collective-permute-start | bytes 6291464 | tf_op jit(solution)/shard_map/ppermute | solution.py:394
  614.0 74.2 %collective-permute-start.17 = (bf16[4,256,1024]{2,1,0:T(8,128)(2,1)}, bf16[4,256,1024]{2,1,0:T(8,128)(2,1)S(1)}, u32[]{:S(2)}, u32[]{:S(2)}) collective-permute-start(bf16[4,256,1024]{2,1,0:T(8,128)(2,1)} %get-tuple-element.37.refs_1_), channel_id=1, source_target_pairs={{0,2},{1,3},{2,4},{3,5},{4,6},{5,7},{6,0},{7,1},{8,10},{9,11},{10,... | collective-permute-start | bytes 6291464 | tf_op jit(solution)/shard_map/ppermute | solution.py:394
  614.0 89.9 %collective-permute-start.20 = (bf16[4,256,1024]{2,1,0:T(8,128)(2,1)}, bf16[4,256,1024]{2,1,0:T(8,128)(2,1)}, u32[]{:S(2)}, u32[]{:S(2)}) collective-permute-start(bf16[4,256,1024]{2,1,0:T(8,128)(2,1)} %get-tuple-element.36.refs_0_), channel_id=1, source_target_pairs={{0,6},{1,7},{2,0},{3,1},{4,2},{5,3},{6,4},{7,5},{8,14},{9,15},{10,... | collective-permute-start | bytes 6291464 | tf_op jit(solution)/shard_map/ppermute | solution.py:394
  617.5 112.9 %collective-permute-start.53 = (bf16[4,256,1024]{2,1,0:T(8,128)(2,1)}, bf16[4,256,1024]{2,1,0:T(8,128)(2,1)}, u32[]{:S(2)}, u32[]{:S(2)}) collective-permute-start(bf16[4,256,1024]{2,1,0:T(8,128)(2,1)} %collective-permute-done.46.refs_0_), channel_id=1, source_target_pairs={{0,1},{1,0},{2,3},{3,2},{4,5},{5,4},{6,7},{7,6},{8,9},{9,8},{10,11... | collective-permute-start | bytes 6291464 | tf_op jit(solution)/shard_map/ppermute | solution.py:394
  643.3 90.0 %collective-permute-start.56 = (bf16[4,256,1024]{2,1,0:T(8,128)(2,1)}, bf16[4,256,1024]{2,1,0:T(8,128)(2,1)S(1)}, u32[]{:S(2)}, u32[]{:S(2)}) collective-permute-start(bf16[4,256,1024]{2,1,0:T(8,128)(2,1)} %collective-permute-done.55.refs_4_), channel_id=1, source_target_pairs={{0,1},{1,0},{2,3},{3,2},{4,5},{5,4},{6,7},{7,6},{8,9},{9,8},{10,11... | collective-permute-start | bytes 6291464 | tf_op jit(solution)/shard_map/ppermute | solution.py:394
  658.9 74.4 %collective-permute-start.57 = (bf16[4,256,1024]{2,1,0:T(8,128)(2,1)}, bf16[4,256,1024]{2,1,0:T(8,128)(2,1)S(1)}, u32[]{:S(2)}, u32[]{:S(2)}) collective-permute-start(bf16[4,256,1024]{2,1,0:T(8,128)(2,1)} %collective-permute-done.48.refs_5_), channel_id=1, source_target_pairs={{0,1},{1,0},{2,3},{3,2},{4,5},{5,4},{6,7},{7,6},{8,9},{9,8},{10,11... | collective-permute-start | bytes 6291464 | tf_op jit(solution)/shard_map/ppermute | solution.py:394
  733.2 78.5 %collective-permute-start.13 = (bf16[3,256,1024]{2,1,0:T(8,128)(2,1)S(1)}, bf16[3,256,1024]{2,1,0:T(8,128)(2,1)}, u32[]{:S(2)}, u32[]{:S(2)}) collective-permute-start(bf16[3,256,1024]{2,1,0:T(8,128)(2,1)S(1)} %slice.18), channel_id=1, source_target_pairs={{0,2},{1,3},{2,4},{3,5},{4,6},{5,7},{6,0},{7,1},{8,10},{9,11},{10,... | collective-permute-start | bytes 4718600 | tf_op jit(solution)/shard_map/ppermute | solution.py:394
  733.4 80.3 %collective-permute-start.39 = (bf16[4,256,1024]{2,1,0:T(8,128)(2,1)}, bf16[4,256,1024]{2,1,0:T(8,128)(2,1)S(1)}, u32[]{:S(2)}, u32[]{:S(2)}) collective-permute-start(bf16[4,256,1024]{2,1,0:T(8,128)(2,1)} %collective-permute-done.30.refs_0_), channel_id=1, source_target_pairs={{0,1},{1,0},{2,3},{3,2},{4,5},{5,4},{6,7},{7,6},{8,9},{9,8},{10,11... | collective-permute-start | bytes 6291464 | tf_op jit(solution)/shard_map/ppermute | solution.py:394
  735.2 78.5 %collective-permute-start.15 = (bf16[3,256,1024]{2,1,0:T(8,128)(2,1)S(1)}, bf16[3,256,1024]{2,1,0:T(8,128)(2,1)}, u32[]{:S(2)}, u32[]{:S(2)}) collective-permute-start(bf16[3,256,1024]{2,1,0:T(8,128)(2,1)S(1)} %slice.19), channel_id=1, source_target_pairs={{0,6},{1,7},{2,0},{3,1},{4,2},{5,3},{6,4},{7,5},{8,14},{9,15},{10,... | collective-permute-start | bytes 4718600 | tf_op jit(solution)/shard_map/ppermute | solution.py:394
  863.9 100.7 %collective-permute-start.21 = (bf16[4,256,1024]{2,1,0:T(8,128)(2,1)}, bf16[4,256,1024]{2,1,0:T(8,128)(2,1)}, u32[]{:S(2)}, u32[]{:S(2)}) collective-permute-start(bf16[4,256,1024]{2,1,0:T(8,128)(2,1)} %collective-permute-done.20.refs_4_), channel_id=1, source_target_pairs={{0,1},{1,0},{2,3},{3,2},{4,5},{5,4},{6,7},{7,6},{8,9},{9,8},{10,11... | collective-permute-start | bytes 6291464 | tf_op jit(solution)/shard_map/ppermute | solution.py:394
  867.0 109.7 %collective-permute-start.14 = (bf16[3,256,1024]{2,1,0:T(8,128)(2,1)}, bf16[3,256,1024]{2,1,0:T(8,128)(2,1)}, u32[]{:S(2)}, u32[]{:S(2)}) collective-permute-start(bf16[3,256,1024]{2,1,0:T(8,128)(2,1)} %collective-permute-done.13.refs_0_), channel_id=1, source_target_pairs={{0,1},{1,0},{2,3},{3,2},{4,5},{5,4},{6,7},{7,6},{8,9},{9,8},{10,11... | collective-permute-start | bytes 4718600 | tf_op jit(solution)/shard_map/ppermute | solution.py:394
  870.0 106.7 %collective-permute-start.16 = (bf16[3,256,1024]{2,1,0:T(8,128)(2,1)}, bf16[3,256,1024]{2,1,0:T(8,128)(2,1)}, u32[]{:S(2)}, u32[]{:S(2)}) collective-permute-start(bf16[3,256,1024]{2,1,0:T(8,128)(2,1)} %collective-permute-done.15.refs_2_), channel_id=1, source_target_pairs={{0,1},{1,0},{2,3},{3,2},{4,5},{5,4},{6,7},{7,6},{8,9},{9,8},{10,11... | collective-permute-start | bytes 4718600 | tf_op jit(solution)/shard_map/ppermute | solution.py:394
  873.0 111.4 %collective-permute-start.12 = (bf16[1,256,1024]{2,1,0:T(8,128)(2,1)}, bf16[1,256,1024]{2,1,0:T(8,128)(2,1)}, u32[]{:S(2)}, u32[]{:S(2)}) collective-permute-start(bf16[1,256,1024]{2,1,0:T(8,128)(2,1)} %collective-permute-done.11.refs_1_), channel_id=1, source_target_pairs={{0,1},{1,0},{2,3},{3,2},{4,5},{5,4},{6,7},{7,6},{8,9},{9,8},{10,11... | collective-permute-start | bytes 1572872 | tf_op jit(solution)/shard_map/ppermute | solution.py:394
  877.3 107.0 %collective-permute-start.9 = (bf16[1,256,1024]{2,1,0:T(8,128)(2,1)}, bf16[1,256,1024]{2,1,0:T(8,128)(2,1)}, u32[]{:S(2)}, u32[]{:S(2)}) collective-permute-start(bf16[1,256,1024]{2,1,0:T(8,128)(2,1)} %collective-permute-done.8.refs_0_), channel_id=1, source_target_pairs={{0,1},{1,0},{2,3},{3,2},{4,5},{5,4},{6,7},{7,6},{8,9},{9,8},{10,11... | collective-permute-start | bytes 1572872 | tf_op jit(solution)/shard_map/ppermute | solution.py:394
  (51 other events, 2187.3 us)

commit v3 on v2

--- a/solution.py
+++ b/solution.py
@@ -23,6 +23,7 @@
 BLK = 256
 CHUNK = 32
 SLOTS = 8
+LAST_ROWS = 32
 VMEM_LIMIT = 67043328
 F32 = jnp.float32
 BF16 = jnp.bfloat16
@@ -47,28 +48,27 @@
 
 
 def greet_group(me, group, chips):
-    barrier = pltpu.get_barrier_semaphore()
     for k in range(group):
         if k != group - CORES:
-            pl.semaphore_signal(barrier, inc=1, device_id={"data": target_of(me, k, chips)}, device_id_type=MESH)
-    pl.semaphore_wait(barrier, group - 1)
+            pl.semaphore_signal(
+                pltpu.get_barrier_semaphore(), inc=1, device_id={"data": target_of(me, k, chips)}, device_id_type=MESH)
 
 
 def newton_schulz(y, gram, poly):
     rows, cols = y.shape
 
+    def fill(target, i, block):
+        target[i:i + BLK, i:] = block
+        for at in range(i + BLK, cols, BLK):
+            target[at:at + BLK, i:i + BLK] = block[:, at - i:at - i + BLK].T
+
     def iteration(_, carry):
-        def gram_block(i, c):
-            at = aligned(i * BLK, BLK)
-            gram[at, :] = lax.dot_general(y[:, at], y[...], (((0,), (0,)), ((), ())), preferred_element_type=F32).astype(BF16)
-            return c
-
-        def poly_block(i, c):
-            at = aligned(i * BLK, BLK)
-            part = gram[at, :]
-            square = jnp.dot(part, gram[...], preferred_element_type=F32)
-            poly[at, :] = (COEF_B * part.astype(F32) + COEF_C * square).astype(BF16)
-            return c
+        for i in range(0, cols, BLK):
+            block = lax.dot_general(y[:, i:i + BLK], y[:, i:], (((0,), (0,)), ((), ())), preferred_element_type=F32)
+            fill(gram, i, block.astype(BF16))
+        for i in range(0, cols, BLK):
+            square = jnp.dot(gram[i:i + BLK, :], gram[:, i:], preferred_element_type=F32)
+            fill(poly, i, (COEF_B * gram[i:i + BLK, i:].astype(F32) + COEF_C * square).astype(BF16))
 
         def update_block(i, c):
             at = aligned(i * BLK, BLK)
@@ -77,8 +77,6 @@
             y[at, :] = (COEF_A * part.astype(F32) + prod).astype(BF16)
             return c
 
-        lax.fori_loop(0, cols // BLK, gram_block, 0)
-        lax.fori_loop(0, cols // BLK, poly_block, 0)
         lax.fori_loop(0, rows // BLK, update_block, 0)
         return carry
 
@@ -252,7 +250,7 @@
     for copy in loads(0):
         copy.start()
 
-    def form(t, c):
+    def form(t):
         @pl.when(t + 1 < steps)
         def _():
             for copy in loads(t + 1):
@@ -279,13 +277,14 @@
             part = part + acc[:, col:col + 128]
         norm_send[at_send] = part
 
-        @pl.when(t > 0)
-        def _():
-            dispatch(t - 1)
-
+    def form_and_send(t, c):
+        form(t)
+        dispatch(t - 1)
         return c
 
-    lax.fori_loop(0, steps, form, 0)
+    form(jnp.int32(0))
+    pl.semaphore_wait(pltpu.get_barrier_semaphore(), group - 1)
+    lax.fori_loop(1, steps, form_and_send, 0)
     start_weights(me, 0, group, w_hbm, w_vmem, w_sem, chips)
 
     def arrived(wave):
@@ -357,17 +356,20 @@
     out, buf, in_sem, out_sem = refs[-4:]
     slots, rows_dev = buf.shape[:2]
     lag = slots // 2
-    steps = [(p, first, o, dx, dc) for p, (first, count, dx, dc) in enumerate(pieces) for o in range(count)]
+    steps = [(p, first, o, dx, dc, row) for p, (first, dx, dc, row) in enumerate(pieces) for o in range(refs[p].shape[0])]
+
+    def slot(t):
+        return buf.at[t % slots, pl.ds(0, refs[steps[t][0]].shape[1])]
 
     def take(t):
-        p, _, o, _, _ = steps[t]
-        return pltpu.make_async_copy(refs[p].at[o], buf.at[t % slots], in_sem.at[t % slots])
+        p, _, o, _, _, _ = steps[t]
+        return pltpu.make_async_copy(refs[p].at[o], slot(t), in_sem.at[t % slots])
 
     def put(t):
-        _, first, o, dx, dc = steps[t]
+        p, first, o, dx, dc, row = steps[t]
         owner_rows = lax.rem(me // CORES + chips - dx, chips) * CORES + lax.rem(lax.rem(me, CORES) + dc, CORES)
-        dst = out.at[wave * group + first + o, aligned(owner_rows * rows_dev, rows_dev)]
-        return pltpu.make_async_copy(buf.at[t % slots], dst, out_sem.at[t % slots])
+        dst = out.at[wave * group + first + o, pl.ds(pl.multiple_of(owner_rows * rows_dev + row, LAST_ROWS), refs[p].shape[1])]
+        return pltpu.make_async_copy(slot(t), dst, out_sem.at[t % slots])
 
     for t in range(len(steps) + lag):
         if t < len(steps):
@@ -471,14 +473,10 @@
         def pass_on(near):
             return shift(near[0], 1, 0), shift(near[3], chips - 1, 0)
 
-        def part_cores(block, first):
-            count = block.shape[0]
-            return (block, first, count, 2, 0), (shift(block, 0, 1), first, count, 2, 1)
-
         def both_cores(pair, dx):
             lo, hi = pair
-            return [(lo, 0, half, dx, 0), (hi, half, half, dx, 0)], [
-                (shift(lo, 0, 1), 0, half, dx, 1), (shift(hi, 0, 1), half, half, dx, 1)
+            return [(lo, 0, dx, 0, 0), (hi, half, dx, 0, 0)], [
+                (shift(lo, 0, 1), 0, dx, 1, 0), (shift(hi, 0, 1), half, dx, 1, 0)
             ]
 
         mom_after = w_lo
@@ -539,15 +537,19 @@
         params = place(params, last, sum(own_p[last], []))
         params = place(params, last - 1, sum(far_p[last - 1], []))
         params = place(params, last, sum(up_p[last] + down_p[last], []))
-        first_part, last_part = [], []
+        placed = {part: [] for part in "abcz"}
         for block, dx, first in ((near[last][0], 1, 0), (near[last][3], chips - 1, half)):
-            cut = half - 1
-            for rows_of, at, part in ((block[:cut], first, first_part), (block[cut:], first + cut, last_part)):
+            cut, row = half - 1, rows_dev - LAST_ROWS
+            pieces = [("a", block[:cut - 1], 0, "a"), ("b", block[cut - 1:cut], cut - 1, "b"), ("c", block[cut:, :row], cut, "z")]
+            for part, rows_of, at, swapped_in in pieces:
                 far_block = shift(rows_of, dx, 0)
-                part.append(part_cores(far_block, at))
-        params = place(params, last, [p for pair in first_part for p in pair])
-        params = place(params, last, [pair[0] for pair in last_part])
-        params = place(params, last, [pair[1] for pair in last_part])
+                placed[part].append((far_block, first + at, 2, 0, 0))
+                placed[swapped_in].append((shift(far_block, 0, 1), first + at, 2, 1, 0))
+            rows_of = block[cut:, row:]
+            placed["z"].append((shift(rows_of, dx, 0), first + cut, 2, 0, row))
+            placed["z"].append((shift(rows_of, dx, 1), first + cut, 2, 1, row))
+        for pieces in placed.values():
+            params = place(params, last, pieces)
         return params, mom_new
 
     return jax.shard_map(local_step, mesh=mesh, in_specs=(row_spec,) * 3, out_specs=(full_spec, row_spec), check_vma=False)

time: 989 us -> 996 us (level)
  Pallas kernels: 464 us -> 428 us
  waiting for transfers between devices: 461 us -> 487 us
  starting transfers between devices: 58.4 us -> 72.8 us
    pallas_call x2, Pallas kernels: 150 us -> 114 us  [local_step(): pl.pallas_call(functools.partial(later_kernel, group, wave), out_shape=(j...]
    ppermute x60 -> x68, waiting for transfers between devices: 461 us -> 487 us  [shift(): return lax.ppermute(block, 'data', pairs)]
    ppermute x60 -> x68, starting transfers between devices: 58.4 us -> 72.8 us  [shift(): return lax.ppermute(block, 'data', pairs)]
    pallas_call x11 -> x12, Pallas kernels: 80.4 us -> 82.2 us  [place(): pl.pallas_call(functools.partial(place_kernel, group, wave, tuple((tuple(...]
  transfers between devices with their start and end apart: 60 -> 68, of which waited for: 29 -> 28; matrix products, arithmetic and copies ran while one was open for 0% -> 0% of each run, Pallas kernels for 20% -> 18%
where the time goes in v3:
time: 996 us; the launch traced here: 994 us
  waiting for transfers between devices  487 us (49%)
  Pallas kernels  428 us (43%)
  starting transfers between devices  72.8 us (7%)
    ppermute x68, waiting for transfers between devices, shift(): return lax.ppermute(block, 'data', pairs)  487 us
    pallas_call x1, Pallas kernels, local_step(): pl.pallas_call(functools.partial(first_kernel, group, waves), name='first...  190 us
    pallas_call x2, Pallas kernels, local_step(): pl.pallas_call(functools.partial(later_kernel, group, wave), out_shape=(j...  114 us
    pallas_call x12, Pallas kernels, place(): pl.pallas_call(functools.partial(place_kernel, group, wave, tuple((tuple(...  82.2 us
    ppermute x68, starting transfers between devices, shift(): return lax.ppermute(block, 'data', pairs)  72.8 us
    pallas_call x1, Pallas kernels, local_step(): pl.pallas_call(momentum_kernel, name='momentum', grid=(mats,), out_shape=...  28.2 us
  transfers between devices with their start and end apart: 68, of which 28 were waited for; matrix products, arithmetic and copies ran while one was open for 0% of the time, Pallas kernels for 18%

profile of v3, /device:TPU:113, one launch (start us, length us, event | category | flops | bytes accessed | tf_op | source)
XLA Modules:
  0.0 993.6 jit_solution(17397701209238290081)
XLA Ops:
  0.6 189.5 %first_wave.1 = (bf16[4,256,1024]{2,1,0:T(8,128)(2,1)}, bf16[4,256,1024]{2,1,0:T(8,128)(2,1)}, bf16[3,2048,1024]{2,1,0:T(8,128)(2,1)}, f32[3,8,8,128]{3,2,1,0:T(8,128)}) custom-call(f32[24,256,1024]{2,1,0:T(8,128)} %mom.3, bf16[24,256,1024]{2,1,0:T(8,128)(2,1)} %grad.3, f32[24,256,1024]{2,1,0:T(8,128)} %refs_8_.3), custom_call_target="tpu_custom_call" | custom-call | flops 53687091200 | bytes 16777216 | tf_op jit(solution)/shard_map/first_wave/pallas_call | solution.py:440
  190.2 57.1 %shard_map.52 = (bf16[256,1024]{1,0:T(8,128)(2,1)}, bf16[256,1024]{1,0:T(8,128)(2,1)}, bf16[256,1024]{1,0:T(8,128)(2,1)}, bf16[256,1024]{1,0:T(8,128)(2,1)}, bf1...) custom-call(bf16[3,2048,1024]{2,1,0:T(8,128)(2,1)} %get-tuple-element, ...), custom_call_target="tpu_custom_call" | custom-call | flops 53687091200 | bytes 16777216 | tf_op jit(solution)/shard_map/pallas_call | solution.py:486
  255.2 7.4 collective-permute-done.31.refs_0_
  265.3 8.6 collective-permute-done.32.refs_1_
  274.3 57.3 %shard_map.50 = (bf16[256,1024]{1,0:T(8,128)(2,1)}, bf16[256,1024]{1,0:T(8,128)(2,1)}, bf16[256,1024]{1,0:T(8,128)(2,1)}, bf16[256,1024]{1,0:T(8,128)(2,1)}, bf1...) custom-call(bf16[3,2048,1024]{2,1,0:T(8,128)(2,1)} %get-tuple-element, ...), custom_call_target="tpu_custom_call" | custom-call | flops 53687091200 | bytes 16777216 | tf_op jit(solution)/shard_map/pallas_call | solution.py:486
  336.0 10.6 %collective-permute-done.refs_0_ = bf16[256,1024]{1,0:T(8,128)(2,1)} collective-permute-done((bf16[256,1024]{1,0:T(8,128)(2,1)}, bf16[256,1024]{1,0:T(8,128)(2,1)}, u32[]{:S(2)}, u32[]{:S(2)}) %collective-permute-start) | collective-permute-done | bytes 524320 | tf_op jit(solution)/shard_map/ppermute | solution.py:396
  346.8 56.7 %collective-permute-done.1.refs_1_ = bf16[256,1024]{1,0:T(8,128)(2,1)} collective-permute-done((bf16[256,1024]{1,0:T(8,128)(2,1)}, bf16[256,1024]{1,0:T(8,128)(2,1)}, u32[]{:S(2)}, u32[]{:S(2)}) %collective-permute-start.1) | collective-permute-done | bytes 524320 | tf_op jit(solution)/shard_map/ppermute | solution.py:396
  404.3 9.8 collective-permute-done.2.refs_2_
  414.1 11.9 %collective-permute-done.3.refs_3_ = bf16[256,1024]{1,0:T(8,128)(2,1)} collective-permute-done((bf16[256,1024]{1,0:T(8,128)(2,1)}, bf16[256,1024]{1,0:T(8,128)(2,1)}, u32[]{:S(2)}, u32[]{:S(2)}) %collective-permute-start.3) | collective-permute-done | bytes 524320 | tf_op jit(solution)/shard_map/ppermute | solution.py:396
  428.7 10.8 %collective-permute-done.5.refs_5_ = bf16[256,1024]{1,0:T(8,128)(2,1)} collective-permute-done((bf16[256,1024]{1,0:T(8,128)(2,1)}, bf16[256,1024]{1,0:T(8,128)(2,1)}, u32[]{:S(2)}, u32[]{:S(2)}) %collective-permute-start.5) | collective-permute-done | bytes 524320 | tf_op jit(solution)/shard_map/ppermute | solution.py:396
  441.5 6.9 shard_map.53
  451.2 36.1 %collective-permute-done.63.refs_4_ = bf16[4,256,1024]{2,1,0:T(8,128)(2,1)} collective-permute-done((bf16[4,256,1024]{2,1,0:T(8,128)(2,1)}, bf16[4,256,1024]{2,1,0:T(8,128)(2,1)}, u32[]{:S(2)}, u32[]{:S(2)}) %collective-permute-start.63) | collective-permute-done | bytes 2097184 | tf_op jit(solution)/shard_map/ppermute | solution.py:396
  487.8 44.5 %collective-permute-done.56.refs_5_ = bf16[4,256,1024]{2,1,0:T(8,128)(2,1)} collective-permute-done((bf16[4,256,1024]{2,1,0:T(8,128)(2,1)}, bf16[4,256,1024]{2,1,0:T(8,128)(2,1)}, u32[]{:S(2)}, u32[]{:S(2)}) %collective-permute-start.56) | collective-permute-done | bytes 2097184 | tf_op jit(solution)/shard_map/ppermute | solution.py:396
  537.4 6.8 shard_map.51
  545.8 33.4 %collective-permute-done.40.refs_5_ = bf16[4,256,1024]{2,1,0:T(8,128)(2,1)} collective-permute-done((bf16[4,256,1024]{2,1,0:T(8,128)(2,1)}, bf16[4,256,1024]{2,1,0:T(8,128)(2,1)}, u32[]{:S(2)}, u32[]{:S(2)}) %collective-permute-start.40) | collective-permute-done | bytes 2097184 | tf_op jit(solution)/shard_map/ppermute | solution.py:396
  589.1 35.0 %collective-permute-done.49.refs_4_ = bf16[4,256,1024]{2,1,0:T(8,128)(2,1)} collective-permute-done((bf16[4,256,1024]{2,1,0:T(8,128)(2,1)}, bf16[4,256,1024]{2,1,0:T(8,128)(2,1)}, u32[]{:S(2)}, u32[]{:S(2)}) %collective-permute-start.49) | collective-permute-done | bytes 2097184 | tf_op jit(solution)/shard_map/ppermute | solution.py:396
  624.3 44.7 %collective-permute-done.12.refs_5_ = bf16[4,256,1024]{2,1,0:T(8,128)(2,1)S(1)} collective-permute-done((bf16[4,256,1024]{2,1,0:T(8,128)(2,1)}, bf16[4,256,1024]{2,1,0:T(8,128)(2,1)S(1)}, u32[]{:S(2)}, u32[]{:S(2)}) %collective-permute-start.12) | collective-permute-done | bytes 2097184 | tf_op jit(solution)/shard_map/ppermute | solution.py:396
  676.2 38.9 %collective-permute-done.28.refs_4_ = bf16[4,256,1024]{2,1,0:T(8,128)(2,1)} collective-permute-done((bf16[4,256,1024]{2,1,0:T(8,128)(2,1)}, bf16[4,256,1024]{2,1,0:T(8,128)(2,1)}, u32[]{:S(2)}, u32[]{:S(2)}) %collective-permute-start.28) | collective-permute-done | bytes 2097184 | tf_op jit(solution)/shard_map/ppermute | solution.py:396
  715.3 6.0 collective-permute-done.10.refs_1_
  728.4 5.8 collective-permute-start.61
  734.3 24.3 %collective-permute-done.19.refs_2_ = bf16[1,256,1024]{2,1,0:T(8,128)(2,1)S(1)} collective-permute-done((bf16[1,256,1024]{2,1,0:T(8,128)(2,1)S(1)}, bf16[1,256,1024]{2,1,0:T(8,128)(2,1)S(1)}, u32[]{:S(2)}, u32[]{:S(2)}) %collective-permute-start.19) | collective-permute-done | bytes 524320 | tf_op jit(solution)/shard_map/ppermute | solution.py:396
  770.2 42.9 %collective-permute-done.55.refs_0_ = bf16[4,256,1024]{2,1,0:T(8,128)(2,1)S(1)} collective-permute-done((bf16[4,256,1024]{2,1,0:T(8,128)(2,1)}, bf16[4,256,1024]{2,1,0:T(8,128)(2,1)S(1)}, u32[]{:S(2)}, u32[]{:S(2)}) %collective-permute-start.55) | collective-permute-done | bytes 2097184 | tf_op jit(solution)/shard_map/ppermute | solution.py:396
  818.6 43.7 %collective-permute-done.39.refs_0_ = bf16[4,256,1024]{2,1,0:T(8,128)(2,1)S(1)} collective-permute-done((bf16[4,256,1024]{2,1,0:T(8,128)(2,1)}, bf16[4,256,1024]{2,1,0:T(8,128)(2,1)S(1)}, u32[]{:S(2)}, u32[]{:S(2)}) %collective-permute-start.39) | collective-permute-done | bytes 2097184 | tf_op jit(solution)/shard_map/ppermute | solution.py:396
  878.2 28.2 %momentum.1 = f32[24,256,1024]{2,1,0:T(8,128)} custom-call(f32[24,256,1024]{2,1,0:T(8,128)} %mom.3, bf16[24,256,1024]{2,1,0:T(8,128)(2,1)} %grad.3, bf16[4,256,1024]{2,1,0:T(8,128)(2,1)} %get-tuple-element.48.refs_0_._), custom_call_target="tpu_custom_call" | custom-call | flops 629145600 | bytes 62914560 | tf_op jit(solution)/shard_map/momentum/pallas_call | solution.py:511
  906.4 6.9 shard_map.54.refs_8_
  914.8 12.1 %shard_map.55.refs_4_ = bf16[24,2048,1024]{2,1,0:T(8,128)(2,1)} custom-call(bf16[4,256,1024]{2,1,0:T(8,128)(2,1)} %collective-permute-done.54.refs_0_, bf16[4,256,1024]{2,1,0:T(8,128)(2,1)} %collective-permute-done.60.refs_1_, bf16[4,256,1024]{2,1,0:T(8,128)(2,1)} %collective-permute-done.61.refs_2_, ...), custom_call_target="tpu_custom_call", output_to_operand_aliasing={{}: (8, {})} | custom-call | flops 335544320 | bytes 33554432 | tf_op jit(solution)/shard_map/pallas_call | solution.py:424
  926.9 6.9 shard_map.56.refs_4_
  933.8 6.9 shard_map.57.refs_8_
  940.6 12.1 %shard_map.58.refs_4_ = bf16[24,2048,1024]{2,1,0:T(8,128)(2,1)} custom-call(bf16[4,256,1024]{2,1,0:T(8,128)(2,1)} %collective-permute-done.38.refs_0_, bf16[4,256,1024]{2,1,0:T(8,128)(2,1)} %collective-permute-done.46.refs_1_, bf16[4,256,1024]{2,1,0:T(8,128)(2,1)} %copy-done.17, ...), custom_call_target="tpu_custom_call", output_to_operand_aliasing={{}: (8, {})} | custom-call | flops 335544320 | bytes 33554432 | tf_op jit(solution)/shard_map/pallas_call | solution.py:424
  952.7 6.9 shard_map.59.refs_4_
  959.6 6.9 shard_map.60.refs_8_
  969.7 12.1 %shard_map.61.refs_4_ = bf16[24,2048,1024]{2,1,0:T(8,128)(2,1)} custom-call(bf16[4,256,1024]{2,1,0:T(8,128)(2,1)} %copy-done.1, bf16[4,256,1024]{2,1,0:T(8,128)(2,1)} %copy-done.12, bf16[4,256,1024]{2,1,0:T(8,128)(2,1)} %copy-done.16, bf16[4,256,1024]{2,1,0:T(8,128)(2,1)} %copy-done.20, ...), custom_call_target="tpu_custom_call", output_to_operand_aliasing={{}: (8, {})} | custom-call | flops 335544320 | bytes 33554432 | tf_op jit(solution)/shard_map/pallas_call | solution.py:424
  (184 shorter events, 104.5 us)
Async XLA Ops:
  249.0 82.6 %collective-permute-start.33 = (bf16[256,1024]{1,0:T(8,128)(2,1)}, bf16[256,1024]{1,0:T(8,128)(2,1)}, u32[]{:S(2)}, u32[]{:S(2)}) collective-permute-start(bf16[256,1024]{1,0:T(8,128)(2,1)} %get-tuple-element.40), channel_id=1, source_target_pairs={{0,4},{1,5},{2,6},{3,7},{4,0},{5,1},{6,2},{7,3},{8,12},{9,13},{10,... | collective-permute-start | bytes 1572872 | tf_op jit(solution)/shard_map/ppermute | solution.py:396
  251.5 80.8 %collective-permute-start.34 = (bf16[256,1024]{1,0:T(8,128)(2,1)}, bf16[256,1024]{1,0:T(8,128)(2,1)}, u32[]{:S(2)}, u32[]{:S(2)}) collective-permute-start(bf16[256,1024]{1,0:T(8,128)(2,1)} %get-tuple-element.41), channel_id=1, source_target_pairs={{0,5},{1,4},{2,7},{3,6},{4,1},{5,0},{6,3},{7,2},{8,13},{9,12},{10,... | collective-permute-start | bytes 1572872 | tf_op jit(solution)/shard_map/ppermute | solution.py:396
  252.7 80.4 %collective-permute-start.35 = (bf16[256,1024]{1,0:T(8,128)(2,1)}, bf16[256,1024]{1,0:T(8,128)(2,1)}, u32[]{:S(2)}, u32[]{:S(2)}) collective-permute-start(bf16[256,1024]{1,0:T(8,128)(2,1)} %get-tuple-element.42), channel_id=1, source_target_pairs={{0,6},{1,7},{2,0},{3,1},{4,2},{5,3},{6,4},{7,5},{8,14},{9,15},{10,... | collective-permute-start | bytes 1572872 | tf_op jit(solution)/shard_map/ppermute | solution.py:396
  262.7 70.5 %collective-permute-start.36 = (bf16[256,1024]{1,0:T(8,128)(2,1)}, bf16[256,1024]{1,0:T(8,128)(2,1)}, u32[]{:S(2)}, u32[]{:S(2)}) collective-permute-start(bf16[256,1024]{1,0:T(8,128)(2,1)} %get-tuple-element.43), channel_id=1, source_target_pairs={{0,7},{1,6},{2,1},{3,0},{4,3},{5,2},{6,5},{7,4},{8,15},{9,14},{10,... | collective-permute-start | bytes 1572872 | tf_op jit(solution)/shard_map/ppermute | solution.py:396
  273.9 59.3 %collective-permute-start.37 = (bf16[256,1024]{1,0:T(8,128)(2,1)}, bf16[256,1024]{1,0:T(8,128)(2,1)}, u32[]{:S(2)}, u32[]{:S(2)}) collective-permute-start(bf16[256,1024]{1,0:T(8,128)(2,1)} %get-tuple-element.45), channel_id=1, source_target_pairs={{0,1},{1,0},{2,3},{3,2},{4,5},{5,4},{6,7},{7,6},{8,9},{9,8},{10,11... | collective-permute-start | bytes 1572872 | tf_op jit(solution)/shard_map/ppermute | solution.py:396
  332.3 116.2 %collective-permute-start.66 = (bf16[4,256,1024]{2,1,0:T(8,128)(2,1)}, bf16[4,256,1024]{2,1,0:T(8,128)(2,1)}, u32[]{:S(2)}, u32[]{:S(2)}) collective-permute-start(bf16[4,256,1024]{2,1,0:T(8,128)(2,1)} %get-tuple-element.48.refs_0_._), channel_id=1, source_target_pairs={{0,1},{1,0},{2,3},{3,2},{4,5},{5,4},{6,7},{7,6},{8,9},{9,8},{10,11... | collective-permute-start | bytes 6291464 | tf_op jit(solution)/shard_map/ppermute | solution.py:396
  333.1 116.8 %collective-permute-start.67 = (bf16[4,256,1024]{2,1,0:T(8,128)(2,1)}, bf16[4,256,1024]{2,1,0:T(8,128)(2,1)}, u32[]{:S(2)}, u32[]{:S(2)}) collective-permute-start(bf16[4,256,1024]{2,1,0:T(8,128)(2,1)} %get-tuple-element.49.refs_1_), channel_id=1, source_target_pairs={{0,1},{1,0},{2,3},{3,2},{4,5},{5,4},{6,7},{7,6},{8,9},{9,8},{10,11... | collective-permute-start | bytes 6291464 | tf_op jit(solution)/shard_map/ppermute | solution.py:396
  333.1 118.0 %collective-permute-start.54 = (bf16[4,256,1024]{2,1,0:T(8,128)(2,1)}, bf16[4,256,1024]{2,1,0:T(8,128)(2,1)}, u32[]{:S(2)}, u32[]{:S(2)}) collective-permute-start(bf16[4,256,1024]{2,1,0:T(8,128)(2,1)} %get-tuple-element.48.refs_0_._), channel_id=1, source_target_pairs={{0,2},{1,3},{2,4},{3,5},{4,6},{5,7},{6,0},{7,1},{8,10},{9,11},{10,... | collective-permute-start | bytes 6291464 | tf_op jit(solution)/shard_map/ppermute | solution.py:396
  333.2 70.3 %collective-permute-start.1 = (bf16[256,1024]{1,0:T(8,128)(2,1)}, bf16[256,1024]{1,0:T(8,128)(2,1)}, u32[]{:S(2)}, u32[]{:S(2)}) collective-permute-start(bf16[256,1024]{1,0:T(8,128)(2,1)} %get-tuple-element.29), channel_id=1, source_target_pairs={{0,3},{1,2},{2,5},{3,4},{4,7},{5,6},{6,1},{7,0},{8,11},{9,10},{10,... | collective-permute-start | bytes 1572872 | tf_op jit(solution)/shard_map/ppermute | solution.py:396
  346.6 67.5 %collective-permute-start.2 = (bf16[256,1024]{1,0:T(8,128)(2,1)}, bf16[256,1024]{1,0:T(8,128)(2,1)}, u32[]{:S(2)}, u32[]{:S(2)}) collective-permute-start(bf16[256,1024]{1,0:T(8,128)(2,1)} %get-tuple-element.30), channel_id=1, source_target_pairs={{0,4},{1,5},{2,6},{3,7},{4,0},{5,1},{6,2},{7,3},{8,12},{9,13},{10,... | collective-permute-start | bytes 1572872 | tf_op jit(solution)/shard_map/ppermute | solution.py:396
  448.3 83.9 %collective-permute-start.56 = (bf16[4,256,1024]{2,1,0:T(8,128)(2,1)}, bf16[4,256,1024]{2,1,0:T(8,128)(2,1)}, u32[]{:S(2)}, u32[]{:S(2)}) collective-permute-start(bf16[4,256,1024]{2,1,0:T(8,128)(2,1)} %get-tuple-element.49.refs_1_), channel_id=1, source_target_pairs={{0,6},{1,7},{2,0},{3,1},{4,2},{5,3},{6,4},{7,5},{8,14},{9,15},{10,... | collective-permute-start | bytes 6291464 | tf_op jit(solution)/shard_map/ppermute | solution.py:396
  448.4 86.3 %collective-permute-start.60 = (bf16[4,256,1024]{2,1,0:T(8,128)(2,1)}, bf16[4,256,1024]{2,1,0:T(8,128)(2,1)}, u32[]{:S(2)}, u32[]{:S(2)}) collective-permute-start(bf16[4,256,1024]{2,1,0:T(8,128)(2,1)} %get-tuple-element.49.refs_1_), channel_id=1, source_target_pairs={{0,2},{1,3},{2,4},{3,5},{4,6},{5,7},{6,0},{7,1},{8,10},{9,11},{10,... | collective-permute-start | bytes 6291464 | tf_op jit(solution)/shard_map/ppermute | solution.py:396
  449.9 84.8 %collective-permute-start.52 = (bf16[4,256,1024]{2,1,0:T(8,128)(2,1)}, bf16[4,256,1024]{2,1,0:T(8,128)(2,1)}, u32[]{:S(2)}, u32[]{:S(2)}) collective-permute-start(bf16[4,256,1024]{2,1,0:T(8,128)(2,1)} %get-tuple-element.46.refs_0_), channel_id=1, source_target_pairs={{0,1},{1,0},{2,3},{3,2},{4,5},{5,4},{6,7},{7,6},{8,9},{9,8},{10,11... | collective-permute-start | bytes 6291464 | tf_op jit(solution)/shard_map/ppermute | solution.py:396
  451.1 93.1 %collective-permute-start.53 = (bf16[4,256,1024]{2,1,0:T(8,128)(2,1)}, bf16[4,256,1024]{2,1,0:T(8,128)(2,1)}, u32[]{:S(2)}, u32[]{:S(2)}) collective-permute-start(bf16[4,256,1024]{2,1,0:T(8,128)(2,1)} %get-tuple-element.47.refs_1_), channel_id=1, source_target_pairs={{0,1},{1,0},{2,3},{3,2},{4,5},{5,4},{6,7},{7,6},{8,9},{9,8},{10,11... | collective-permute-start | bytes 6291464 | tf_op jit(solution)/shard_map/ppermute | solution.py:396
  487.3 57.0 %collective-permute-start.38 = (bf16[4,256,1024]{2,1,0:T(8,128)(2,1)}, bf16[4,256,1024]{2,1,0:T(8,128)(2,1)}, u32[]{:S(2)}, u32[]{:S(2)}) collective-permute-start(bf16[4,256,1024]{2,1,0:T(8,128)(2,1)} %get-tuple-element.46.refs_0_), channel_id=1, source_target_pairs={{0,2},{1,3},{2,4},{3,5},{4,6},{5,7},{6,0},{7,1},{8,10},{9,11},{10,... | collective-permute-start | bytes 6291464 | tf_op jit(solution)/shard_map/ppermute | solution.py:396
  534.7 51.7 %collective-permute-start.46 = (bf16[4,256,1024]{2,1,0:T(8,128)(2,1)}, bf16[4,256,1024]{2,1,0:T(8,128)(2,1)}, u32[]{:S(2)}, u32[]{:S(2)}) collective-permute-start(bf16[4,256,1024]{2,1,0:T(8,128)(2,1)} %get-tuple-element.47.refs_1_), channel_id=1, source_target_pairs={{0,2},{1,3},{2,4},{3,5},{4,6},{5,7},{6,0},{7,1},{8,10},{9,11},{10,... | collective-permute-start | bytes 6291464 | tf_op jit(solution)/shard_map/ppermute | solution.py:396
  534.7 89.4 %collective-permute-start.49 = (bf16[4,256,1024]{2,1,0:T(8,128)(2,1)}, bf16[4,256,1024]{2,1,0:T(8,128)(2,1)}, u32[]{:S(2)}, u32[]{:S(2)}) collective-permute-start(bf16[4,256,1024]{2,1,0:T(8,128)(2,1)} %get-tuple-element.46.refs_0_), channel_id=1, source_target_pairs={{0,6},{1,7},{2,0},{3,1},{4,2},{5,3},{6,4},{7,5},{8,14},{9,15},{10,... | collective-permute-start | bytes 6291464 | tf_op jit(solution)/shard_map/ppermute | solution.py:396
  544.2 124.8 %collective-permute-start.12 = (bf16[4,256,1024]{2,1,0:T(8,128)(2,1)}, bf16[4,256,1024]{2,1,0:T(8,128)(2,1)S(1)}, u32[]{:S(2)}, u32[]{:S(2)}) collective-permute-start(bf16[4,256,1024]{2,1,0:T(8,128)(2,1)} %get-tuple-element.37.refs_1_), channel_id=1, source_target_pairs={{0,6},{1,7},{2,0},{3,1},{4,2},{5,3},{6,4},{7,5},{8,14},{9,15},{10,... | collective-permute-start | bytes 6291464 | tf_op jit(solution)/shard_map/ppermute | solution.py:396
  544.4 127.6 %collective-permute-start.7 = (bf16[4,256,1024]{2,1,0:T(8,128)(2,1)}, bf16[4,256,1024]{2,1,0:T(8,128)(2,1)S(1)}, u32[]{:S(2)}, u32[]{:S(2)}) collective-permute-start(bf16[4,256,1024]{2,1,0:T(8,128)(2,1)} %get-tuple-element.36.refs_0_), channel_id=1, source_target_pairs={{0,2},{1,3},{2,4},{3,5},{4,6},{5,7},{6,0},{7,1},{8,10},{9,11},{10,... | collective-permute-start | bytes 6291464 | tf_op jit(solution)/shard_map/ppermute | solution.py:396
  579.2 93.0 %collective-permute-start.44 = (bf16[4,256,1024]{2,1,0:T(8,128)(2,1)}, bf16[4,256,1024]{2,1,0:T(8,128)(2,1)S(1)}, u32[]{:S(2)}, u32[]{:S(2)}) collective-permute-start(bf16[4,256,1024]{2,1,0:T(8,128)(2,1)} %get-tuple-element.36.refs_0_), channel_id=1, source_target_pairs={{0,1},{1,0},{2,3},{3,2},{4,5},{5,4},{6,7},{7,6},{8,9},{9,8},{10,11... | collective-permute-start | bytes 6291464 | tf_op jit(solution)/shard_map/ppermute | solution.py:396
  586.4 87.3 %collective-permute-start.45 = (bf16[4,256,1024]{2,1,0:T(8,128)(2,1)}, bf16[4,256,1024]{2,1,0:T(8,128)(2,1)S(1)}, u32[]{:S(2)}, u32[]{:S(2)}) collective-permute-start(bf16[4,256,1024]{2,1,0:T(8,128)(2,1)} %get-tuple-element.37.refs_1_), channel_id=1, source_target_pairs={{0,1},{1,0},{2,3},{3,2},{4,5},{5,4},{6,7},{7,6},{8,9},{9,8},{10,11... | collective-permute-start | bytes 6291464 | tf_op jit(solution)/shard_map/ppermute | solution.py:396
  624.1 52.1 %collective-permute-start.25 = (bf16[4,256,1024]{2,1,0:T(8,128)(2,1)}, bf16[4,256,1024]{2,1,0:T(8,128)(2,1)S(1)}, u32[]{:S(2)}, u32[]{:S(2)}) collective-permute-start(bf16[4,256,1024]{2,1,0:T(8,128)(2,1)} %get-tuple-element.37.refs_1_), channel_id=1, source_target_pairs={{0,2},{1,3},{2,4},{3,5},{4,6},{5,7},{6,0},{7,1},{8,10},{9,11},{10,... | collective-permute-start | bytes 6291464 | tf_op jit(solution)/shard_map/ppermute | solution.py:396
  672.0 52.9 %collective-permute-start.13 = (bf16[1,224,1024]{2,1,0:T(8,128)(2,1)S(1)}, bf16[1,224,1024]{2,1,0:T(8,128)(2,1)}, u32[]{:S(2)}, u32[]{:S(2)}) collective-permute-start(bf16[1,224,1024]{2,1,0:T(8,128)(2,1)S(1)} %slice.34), channel_id=1, source_target_pairs={{0,6},{1,7},{2,0},{3,1},{4,2},{5,3},{6,4},{7,5},{8,14},{9,15},{10,... | collective-permute-start | bytes 1376264 | tf_op jit(solution)/shard_map/ppermute | solution.py:396
  672.2 89.3 %collective-permute-start.21 = (bf16[2,256,1024]{2,1,0:T(8,128)(2,1)S(1)}, bf16[2,256,1024]{2,1,0:T(8,128)(2,1)}, u32[]{:S(2)}, u32[]{:S(2)}) collective-permute-start(bf16[2,256,1024]{2,1,0:T(8,128)(2,1)S(1)} %slice.38), channel_id=1, source_target_pairs={{0,2},{1,3},{2,4},{3,5},{4,6},{5,7},{6,0},{7,1},{8,10},{9,11},{10,... | collective-permute-start | bytes 3145736 | tf_op jit(solution)/shard_map/ppermute | solution.py:396
  673.8 60.4 %collective-permute-start.17 = (bf16[1,256,1024]{2,1,0:T(8,128)(2,1)S(1)}, bf16[1,256,1024]{2,1,0:T(8,128)(2,1)S(1)}, u32[]{:S(2)}, u32[]{:S(2)}) collective-permute-start(bf16[1,256,1024]{2,1,0:T(8,128)(2,1)S(1)} %slice.36), channel_id=1, source_target_pairs={{0,2},{1,3},{2,4},{3,5},{4,6},{5,7},{6,0},{7,1},{8,10},{9,11},{10,... | collective-permute-start | bytes 1572872 | tf_op jit(solution)/shard_map/ppermute | solution.py:396
  676.2 52.2 %collective-permute-start.8 = (bf16[1,224,1024]{2,1,0:T(8,128)(2,1)S(1)}, bf16[1,224,1024]{2,1,0:T(8,128)(2,1)}, u32[]{:S(2)}, u32[]{:S(2)}) collective-permute-start(bf16[1,224,1024]{2,1,0:T(8,128)(2,1)S(1)} %slice.32), channel_id=1, source_target_pairs={{0,2},{1,3},{2,4},{3,5},{4,6},{5,7},{6,0},{7,1},{8,10},{9,11},{10,... | collective-permute-start | bytes 1376264 | tf_op jit(solution)/shard_map/ppermute | solution.py:396
  764.6 49.4 %collective-permute-start.57 = (bf16[4,256,1024]{2,1,0:T(8,128)(2,1)}, bf16[4,256,1024]{2,1,0:T(8,128)(2,1)S(1)}, u32[]{:S(2)}, u32[]{:S(2)}) collective-permute-start(bf16[4,256,1024]{2,1,0:T(8,128)(2,1)} %collective-permute-done.56.refs_5_), channel_id=1, source_target_pairs={{0,6},{1,7},{2,0},{3,1},{4,2},{5,3},{6,4},{7,5},{8,14},{9,15},{10,... | collective-permute-start | bytes 6291464 | tf_op jit(solution)/shard_map/ppermute | solution.py:396
  864.4 102.1 %collective-permute-start.29 = (bf16[4,256,1024]{2,1,0:T(8,128)(2,1)}, bf16[4,256,1024]{2,1,0:T(8,128)(2,1)}, u32[]{:S(2)}, u32[]{:S(2)}) collective-permute-start(bf16[4,256,1024]{2,1,0:T(8,128)(2,1)} %collective-permute-done.28.refs_4_), channel_id=1, source_target_pairs={{0,1},{1,0},{2,3},{3,2},{4,5},{5,4},{6,7},{7,6},{8,9},{9,8},{10,11... | collective-permute-start | bytes 6291464 | tf_op jit(solution)/shard_map/ppermute | solution.py:396
  867.4 99.2 %collective-permute-start.22 = (bf16[2,256,1024]{2,1,0:T(8,128)(2,1)}, bf16[2,256,1024]{2,1,0:T(8,128)(2,1)}, u32[]{:S(2)}, u32[]{:S(2)}) collective-permute-start(bf16[2,256,1024]{2,1,0:T(8,128)(2,1)} %collective-permute-done.21.refs_0_), channel_id=1, source_target_pairs={{0,1},{1,0},{2,3},{3,2},{4,5},{5,4},{6,7},{7,6},{8,9},{9,8},{10,11... | collective-permute-start | bytes 3145736 | tf_op jit(solution)/shard_map/ppermute | solution.py:396
  870.4 98.9 %collective-permute-start.24 = (bf16[2,256,1024]{2,1,0:T(8,128)(2,1)}, bf16[2,256,1024]{2,1,0:T(8,128)(2,1)}, u32[]{:S(2)}, u32[]{:S(2)}) collective-permute-start(bf16[2,256,1024]{2,1,0:T(8,128)(2,1)} %collective-permute-done.23.refs_2_), channel_id=1, source_target_pairs={{0,1},{1,0},{2,3},{3,2},{4,5},{5,4},{6,7},{7,6},{8,9},{9,8},{10,11... | collective-permute-start | bytes 3145736 | tf_op jit(solution)/shard_map/ppermute | solution.py:396
  873.4 117.3 %collective-permute-start.14 = (bf16[1,224,1024]{2,1,0:T(8,128)(2,1)}, bf16[1,224,1024]{2,1,0:T(8,128)(2,1)}, u32[]{:S(2)}, u32[]{:S(2)}) collective-permute-start(bf16[1,224,1024]{2,1,0:T(8,128)(2,1)} %collective-permute-done.13.refs_1_), channel_id=1, source_target_pairs={{0,1},{1,0},{2,3},{3,2},{4,5},{5,4},{6,7},{7,6},{8,9},{9,8},{10,11... | collective-permute-start | bytes 1376264 | tf_op jit(solution)/shard_map/ppermute | solution.py:396
  877.8 112.9 %collective-permute-start.9 = (bf16[1,224,1024]{2,1,0:T(8,128)(2,1)}, bf16[1,224,1024]{2,1,0:T(8,128)(2,1)}, u32[]{:S(2)}, u32[]{:S(2)}) collective-permute-start(bf16[1,224,1024]{2,1,0:T(8,128)(2,1)} %collective-permute-done.8.refs_0_), channel_id=1, source_target_pairs={{0,1},{1,0},{2,3},{3,2},{4,5},{5,4},{6,7},{7,6},{8,9},{9,8},{10,11... | collective-permute-start | bytes 1376264 | tf_op jit(solution)/shard_map/ppermute | solution.py:396
  (63 other events, 2446.5 us)
